TPU v7x, 512 devices: a 8x2x16 block of a 8x16x16 slice. The times are simulated.
512 devices in a mesh: grp: 2 (over y), ka: 16 (over z), ga: 8 (over x), ba: 2 (over core).
Axes of the slice: x: 8, y: 2, z: 16, core: 2. Of those that a mesh axis runs over, the one named last changes fastest.
The devices are a block of a 8x16x16 slice.
Arguments:
- coefficients: bfloat16 [2, 2, 64, 512, 9216], P(None, None, ('grp', 'ka'), 'ba', 'ga'), parts along dimension 2, may hold values from -1 to 1
- occupied: int32 [2, 64], P(None, ('grp', 'ka')), parts along dimension 1, may hold values from 64 to 512
- kweights: float32 [64], P(('grp', 'ka')), parts along dimension 0, may hold values from 0.5 to 2
- owner_map: int32 [1024], P('grp'), parts along dimension 0, may hold values from 0 to 31, as said below
- species: int32 [1024], P('grp'), parts along dimension 0, may hold values from 0 to 1
- positions: float32 [3, 1024], P(None, 'grp'), parts along dimension 1, may hold values from 0 to 100
- multipole: float32 [2, 9, 324], replicated, may hold values from -0.3125 to 0.3125
- widths: float32 [2], replicated, may hold values from 0.05 to 0.3
- potential: float32 [2, 1769472], P(None, ('grp', 'ga')), parts along dimension 1, may hold values from -0.0068359375 to 0.0068359375
Outputs:
- density: float32 [2, 2, 1024, 324], P(None, None, ('grp', 'ka', 'ga', 'ba')), parts along dimension 2
- forces: float32 [3, 1024], P(None, ('grp', 'ka', 'ga', 'ba')), parts along dimension 1
There are 2 independent parts, one for each index of `grp`. A program takes and returns all parts, laid end to end along the dimension named above; an argument that names none is the same for every part. Nothing has to cross between parts.
Inputs may be any that keep to these rules, and one draw needn't show every extreme that they name: `owner_map`: within each aligned block of 64 atoms every owner number is named by exactly 2 atoms.
All inputs are finite; a program needn't handle non-finite values.
Results may differ from a plain program's by a relative error of at most 0.0003.
Values sent between devices are 32-bit elements; how exact they have to be, the bound alone decides.
No kernel may reach another device: no remote copies, remote signals or barrier semaphores. Data moves between devices by JAX's collectives and lax.ppermute only.
A program may use at most 64 MiB of HBM per device.

v0:
```python
import jax
import jax.numpy as jnp
from jax import lax
from jax.sharding import PartitionSpec as P

NPROJ = 18
SPECIES = 2
NL = 9
GRID = 96


grid_step = 0.0625
highest = lax.Precision.HIGHEST


def cut_along(array, dim, size):
    lengths = array.shape
    tiles = array.reshape(*lengths[:dim], size, lengths[dim] // size, *lengths[dim + 1 :])
    return jnp.moveaxis(tiles, dim, 0)


def sent_and_summed(array, axis, dim):
    tiles = cut_along(array, dim, lax.axis_size(axis))
    arrived = lax.all_to_all(tiles, axis, split_axis=0, concat_axis=0, tiled=True)
    return arrived.sum(axis=0)


def joined_along(tiles, dim):
    tiles = jnp.moveaxis(tiles, 0, dim)
    lengths = tiles.shape
    return tiles.reshape(*lengths[:dim], lengths[dim] * lengths[dim + 1], *lengths[dim + 2 :])


def from_everyone(array, axis):
    copies = jnp.broadcast_to(array, (lax.axis_size(axis), *array.shape))
    return lax.all_to_all(copies, axis, split_axis=0, concat_axis=0, tiled=True)


def gathered_copies(array, axis, dim):
    return joined_along(from_everyone(array, axis), dim)


def over_copies(array, axis):
    return from_everyone(array, axis).sum(axis=0)


def harmonics(start_index, length, widths):
    indices = start_index + jnp.arange(length, dtype=jnp.int32)
    planes = [indices % GRID, indices // GRID % GRID, indices // (GRID * GRID)]
    vectors = []
    for plane_index in planes:
        signed = jnp.where(plane_index >= GRID // 2, plane_index - GRID, plane_index)
        vectors.append(grid_step * signed.astype(jnp.float32))
    along_x, along_y, along_z = vectors
    square = along_x * along_x + along_y * along_y + along_z * along_z
    shapes = jnp.stack(
        [
            jnp.ones_like(square),
            along_x,
            along_y,
            along_z,
            along_x * along_y,
            along_y * along_z,
            along_z * along_x,
            along_x * along_x - along_y * along_y,
            3.0 * along_z * along_z - square,
        ]
    )
    damping = jnp.exp(-widths[:, None] * square[None, :])
    form_table = (damping[:, None, :] * shapes[None, :, :]).reshape(SPECIES * NL, length)
    return (form_table, jnp.stack(vectors, axis=1))


def force_block(moments, places, form_table, vectors, pot_piece):
    smooth = jnp.dot(moments, form_table, precision=highest)
    phases = jnp.dot(places, vectors.T, precision=highest)
    wave_term = pot_piece[0][None, :] * jnp.sin(phases) + pot_piece[1][None, :] * jnp.cos(phases)
    return jnp.dot(smooth * wave_term, vectors, precision=highest)


def local_force(moments, places, pot_piece, start_index, widths):
    length = pot_piece.shape[1]
    pieces = 8
    width_block = length // pieces

    def gblock(running, number):
        offset = number * width_block
        form_table, vectors = harmonics(start_index + offset, width_block, widths)
        segment = lax.dynamic_slice_in_dim(pot_piece, offset, width_block, 1)
        return (running + force_block(moments, places, form_table, vectors, segment), None)

    result, unused = lax.scan(
        gblock, jnp.zeros((moments.shape[0], 3), jnp.float32), jnp.arange(pieces, dtype=jnp.int32)
    )
    return result


def shards(
    coefficients, occupied, kweights, owner_map, species, positions, multipole, widths, potential
):
    spin_count, complex_parts, kcount, bcount, columns = coefficients.shape
    atoms_blk = columns // NPROJ
    kgroups = lax.axis_size("ka")
    bgroups = lax.axis_size("ba")
    owners = kgroups * bgroups
    per_owner = atoms_blk // owners
    owner_index = lax.axis_index(("ka", "ba"))
    group_index = lax.axis_index("ga")
    band_index = lax.axis_index("ba") * bcount + jnp.arange(bcount, dtype=jnp.int32)
    band_mask = (band_index[None, None, :] < occupied[:, :, None]).astype(jnp.bfloat16)
    values = coefficients.reshape(spin_count, complex_parts, kcount, bcount, atoms_blk, NPROJ)
    masked = values * band_mask[:, None, :, :, None, None]
    real_part = jnp.einsum(
        "sckbai,sckbaj->skaij", values, masked, preferred_element_type=jnp.float32
    )
    cross_term = jnp.einsum(
        "skbai,skbaj->skaij", values[:, 0], masked[:, 1], preferred_element_type=jnp.float32
    )
    imag_part = cross_term - jnp.swapaxes(cross_term, 3, 4)
    weighted = jnp.stack([real_part, imag_part], axis=1) * kweights[None, None, :, None, None, None]
    density_local = jnp.sum(weighted, axis=2).reshape(
        spin_count, complex_parts, atoms_blk, NPROJ * NPROJ
    )
    ranking = jnp.argsort(owner_map.reshape(-1, atoms_blk), axis=1, stable=True)
    own_ranks = lax.dynamic_slice_in_dim(ranking, owner_index * per_owner, per_owner, 1)
    group_rows = lax.dynamic_index_in_dim(ranking, group_index, 0, keepdims=False)
    core_rows = jnp.transpose(group_rows.reshape(kgroups, bgroups, per_owner), (1, 0, 2)).reshape(
        -1
    )
    arranged = jnp.take(density_local, core_rows, axis=2)
    core_part = sent_and_summed(arranged, "ba", 2)
    own_density = sent_and_summed(core_part, "ka", 2)
    block_count = own_ranks.shape[0]
    atom_ids = jnp.arange(block_count, dtype=jnp.int32)[:, None] * atoms_blk + own_ranks
    own_atoms = lax.dynamic_index_in_dim(atom_ids, group_index, 0, keepdims=False)
    real_total = jnp.sum(own_density[:, 0], axis=0)
    selector = (
        jnp.take(species, own_atoms)[:, None] == jnp.arange(SPECIES, dtype=jnp.int32)[None, :]
    ).astype(jnp.float32)
    moments = jnp.dot(
        real_total, multipole.reshape(SPECIES * NL, NPROJ * NPROJ).T, precision=highest
    ) * jnp.repeat(selector, NL, axis=1)
    gcount = potential.shape[1]
    all_moments = gathered_copies(moments, "ga", 0)
    places = jnp.take(positions, atom_ids.reshape(-1), axis=1).T
    partial_force = local_force(all_moments, places, potential, group_index * gcount, widths)
    summed_force = over_copies(partial_force, "ga")
    own_force = lax.dynamic_slice_in_dim(summed_force, group_index * per_owner, per_owner, 0)
    return (own_density, own_force.T)


def solution(mesh):
    placed = (
        P(None, None, ("grp", "ka"), "ba", "ga"),
        P(None, ("grp", "ka")),
        P(("grp", "ka")),
        P("grp"),
        P("grp"),
        P(None, "grp"),
        P(),
        P(),
        P(None, ("grp", "ga")),
    )
    return jax.shard_map(
        shards,
        mesh=mesh,
        in_specs=placed,
        out_specs=(
            P(None, None, ("grp", "ka", "ga", "ba"), None),
            P(None, ("grp", "ka", "ga", "ba")),
        ),
        check_vma=False,
    )
```

profile of v0, /device:TPU:80, one launch (start us, length us, event | category | flops | bytes accessed | tf_op | source)
XLA Modules:
  0.0 273.7 jit_solution(13921023420807064290)
XLA Ops:
  3.1 12.4 %copy.74 = bf16[2,2,2,256,1152]{3,2,4,1,0:T(2,128)(2,1)} copy(bf16[2,2,2,256,1152]{4,3,2,1,0:T(8,128)(2,1)} %param.11) | data formatting | bytes 9437184 | tf_op args[0]
  15.6 8.0 %broadcast_multiply_fusion.2 = (bf16[2,2,2,256,64,18]{3,5,4,2,0,1:T(8,128)(2,1)}, bf16[2,2,2,256,64,18]{3,5,4,2,0,1:T(8,128)(2,1)}) fusion(bf16[2,2,256]{2,1,0:T(2,128)(2,1)S(1)} %compare_convert_fusion, bf16[2,2,2,256,64,18]{3,2,5,4,1,0:T(2,128)(2,1)} %bitcast.64), kind=kLoop, calls=%fused_computation.86 | loop fusion | flops 2359296 | bytes 14157824 | tf_op jit(solution)/shard_map/mul | solution.py:112
  23.6 6.7 %fusion.38 = f32[2,2,64,18,18,1]{4,3,0,2,1,5:T(8,128)} fusion(bf16[2,2,2,256,64,18]{3,2,5,4,1,0:T(2,128)(2,1)S(1)} %bitcast.65, bf16[2,2,2,256,64,18]{3,5,4,2,0,1:T(8,128)(2,1)} %get-tuple-element.251), kind=kOutput, calls=%fused_computation.77 | convolution fusion | flops 84934656 | bytes 9768960 | tf_op jit(solution)/shard_map/sckbai,sckbaj->skaij/dot_general | solution.py:113
  30.3 4.0 %fusion.41 = f32[2,2,64,18,18]{4,3,2,1,0:T(8,128)S(1)} fusion(bf16[2,2,2,256,64,18]{3,5,4,2,0,1:T(8,128)(2,1)} %get-tuple-element.252, bf16[2,2,2,256,64,18]{3,5,4,2,0,1:T(8,128)(2,1)} %get-tuple-element.251), kind=kOutput, calls=%fused_computation.81 | convolution fusion | flops 42467328 | bytes 6623232 | tf_op jit(solution)/shard_map/skbai,skbaj->skaij/dot_general | solution.py:116
  34.3 3.1 %copy.78 = f32[2,2,64,18,18]{3,4,2,1,0:T(8,128)} copy(f32[2,2,64,18,18]{4,3,2,1,0:T(8,128)S(1)} %fusion.41) | data formatting | bytes 663552 | tf_op jit(solution)/shard_map/skbai,skbaj->skaij/dot_general | solution.py:116
  37.4 4.1 %fusion.42 = f32[2,1,2,64,18,18]{5,4,3,2,0,1:T(8,128)} fusion(f32[2,2,64,18,18]{4,3,2,1,0:T(8,128)S(1)} %fusion.41, f32[2,2,64,18,18]{3,4,2,1,0:T(8,128)} %copy.78), kind=kLoop, calls=%fused_computation.84 | loop fusion | flops 82944 | bytes 995328 | tf_op jit(solution)/shard_map/stack | solution.py:120
  41.4 3.0 %copy.80 = f32[2,1,2,64,18,18]{3,2,5,4,1,0:T(2,128)} copy(f32[2,1,2,64,18,18]{5,4,3,2,0,1:T(8,128)} %fusion.42) | data formatting | bytes 663552 | tf_op jit(solution)/shard_map/stack | solution.py:120
  44.4 2.1 copy.106
  46.6 1.8 copy.79
  48.3 3.5 %fusion.43 = f32[2,2,64,18,18]{2,4,3,1,0:T(8,128)S(1)} fusion(f32[2,1,2,64,18,18]{3,2,5,4,1,0:T(2,128)} %copy.80, f32[2,1,2,64,18,18]{3,2,5,4,1,0:T(2,128)} %copy.79, f32[2]{0:T(128)S(1)} %copy-done.6), kind=kLoop, calls=%fused_computation.88 | loop fusion | flops 414720 | bytes 995336 | tf_op jit(solution)/shard_map/reduce_sum | solution.py:121
  54.0 4.1 %all_to_all.20 = f32[2,2,2,32,324]{4,2,1,3,0:T(2,128)S(1)} all-to-all(f32[2,2,2,32,324]{4,2,1,3,0:T(2,128)S(1)} %select_bitcast_fusion), channel_id=1, replica_groups=mesh['grp'=2,'ka'=16,'ga'=8,'ba'=2] {'ba'}, dimensions={0} | all-to-all | bytes 663552 | tf_op jit(solution)/shard_map/all_to_all | solution.py:24
  59.2 43.7 %all-to-all-start.1 = ((f32[16,2,2,2,324]{4,3,2,1,0:T(2,128)}), f32[16,2,2,2,324]{4,3,2,1,0:T(2,128)S(1)}, u32[]{:S(2)}, u32[]{:S(2)}) async-start(f32[16,2,2,2,324]{4,3,2,1,0:T(2,128)} %bitcast.51), calls=%async_computation.1 | async-start | bytes 393216 | tf_op jit(solution)/shard_map/all_to_all | solution.py:24
  105.1 13.3 %all-to-all-done.1 = f32[16,2,2,2,324]{4,3,2,1,0:T(2,128)S(1)} async-done(((f32[16,2,2,2,324]{4,3,2,1,0:T(2,128)}), f32[16,2,2,2,324]{4,3,2,1,0:T(2,128)S(1)}, u32[]{:S(2)}, u32[]{:S(2)}) %all-to-all-start.1) | async-done | bytes 165920 | tf_op jit(solution)/shard_map/all_to_all | solution.py:24
  119.3 7.5 %all-to-all-start.2 = ((f32[8,2,18]{2,1,0:T(2,128)}), f32[8,2,18]{2,1,0:T(2,128)S(1)}, u32[]{:S(2)}, u32[]{:S(2)}) async-start(f32[8,2,18]{2,1,0:T(2,128)} %broadcast_in_dim.49), calls=%async_computation.2 | async-start | bytes 16384 | tf_op jit(solution)/shard_map/all_to_all | solution.py:36
  126.9 7.6 %all-to-all-done.2 = f32[8,2,18]{2,1,0:T(2,128)S(1)} async-done(((f32[8,2,18]{2,1,0:T(2,128)}), f32[8,2,18]{2,1,0:T(2,128)S(1)}, u32[]{:S(2)}, u32[]{:S(2)}) %all-to-all-start.2) | async-done | bytes 1184 | tf_op jit(solution)/shard_map/all_to_all | solution.py:36
  134.5 126.7 %while.14 = (s32[]{:T(128)}, f32[16,3]{0,1:T(4,128)S(1)}, f32[2,1]{0,1:T(1,128)S(1)}, s32[8]{0:T(128)S(1)}, s32[]{:T(128)}, /*index=5*/f32[16,18]{1,0:T(8,128)S(...) while((s32[]{:T(128)}, f32[16,3]{0,1:T(4,128)S(1)}, ...), condition=%wide.region_6.7_spmd.clone, body=%wide.region_5.6_spmd.clone.sunk | while | flops 68345960 | bytes 10674137 | solution.py:92
  138.8 1.2 add_subtract_fusion.2
  143.6 1.3 dynamic-slice_reduce_fusion.5
  144.9 4.2 %convolution_multiply_fusion.3 = f32[13824,16]{0,1:T(8,128)S(1)} fusion(f32[18,13824]{1,0:T(8,128)S(1)} %mul.710, f32[16,18]{1,0:T(8,128)S(1)} %get-tuple-element.359, f32[13824,16]{0,1:T(8,128)S(1)} %fusion.72, f32[13824]{0:T(1024)S(1)} %get-tuple-element.324, f32[13824]{0:T(1024)S(1)} %get-tuple-element.325), kind=kOutput, calls=%fused_computation.3.clone.1 | convolution fusion | flops 48660480 | bytes 2876544 | tf_op jit(solution)/shard_map/while/body/eval_jaxpr/dot_general | solution.py:75
  149.1 1.2 convolution_add_fusion.2
  154.6 1.2 add_subtract_fusion.2
  159.4 1.3 dynamic-slice_reduce_fusion.5
  160.8 4.2 %convolution_multiply_fusion.3 = f32[13824,16]{0,1:T(8,128)S(1)} fusion(f32[18,13824]{1,0:T(8,128)S(1)} %mul.710, f32[16,18]{1,0:T(8,128)S(1)} %get-tuple-element.359, f32[13824,16]{0,1:T(8,128)S(1)} %fusion.72, f32[13824]{0:T(1024)S(1)} %get-tuple-element.324, f32[13824]{0:T(1024)S(1)} %get-tuple-element.325), kind=kOutput, calls=%fused_computation.3.clone.1 | convolution fusion | flops 48660480 | bytes 2876544 | tf_op jit(solution)/shard_map/while/body/eval_jaxpr/dot_general | solution.py:75
  165.0 1.2 convolution_add_fusion.2
  170.4 1.2 add_subtract_fusion.2
  175.3 1.3 dynamic-slice_reduce_fusion.5
  176.6 4.2 %convolution_multiply_fusion.3 = f32[13824,16]{0,1:T(8,128)S(1)} fusion(f32[18,13824]{1,0:T(8,128)S(1)} %mul.710, f32[16,18]{1,0:T(8,128)S(1)} %get-tuple-element.359, f32[13824,16]{0,1:T(8,128)S(1)} %fusion.72, f32[13824]{0:T(1024)S(1)} %get-tuple-element.324, f32[13824]{0:T(1024)S(1)} %get-tuple-element.325), kind=kOutput, calls=%fused_computation.3.clone.1 | convolution fusion | flops 48660480 | bytes 2876544 | tf_op jit(solution)/shard_map/while/body/eval_jaxpr/dot_general | solution.py:75
  180.8 1.2 convolution_add_fusion.2
  186.3 1.2 add_subtract_fusion.2
  191.1 1.3 dynamic-slice_reduce_fusion.5
  192.4 4.2 %convolution_multiply_fusion.3 = f32[13824,16]{0,1:T(8,128)S(1)} fusion(f32[18,13824]{1,0:T(8,128)S(1)} %mul.710, f32[16,18]{1,0:T(8,128)S(1)} %get-tuple-element.359, f32[13824,16]{0,1:T(8,128)S(1)} %fusion.72, f32[13824]{0:T(1024)S(1)} %get-tuple-element.324, f32[13824]{0:T(1024)S(1)} %get-tuple-element.325), kind=kOutput, calls=%fused_computation.3.clone.1 | convolution fusion | flops 48660480 | bytes 2876544 | tf_op jit(solution)/shard_map/while/body/eval_jaxpr/dot_general | solution.py:75
  196.6 1.2 convolution_add_fusion.2
  202.1 1.2 add_subtract_fusion.2
  207.0 1.3 dynamic-slice_reduce_fusion.5
  208.3 4.2 %convolution_multiply_fusion.3 = f32[13824,16]{0,1:T(8,128)S(1)} fusion(f32[18,13824]{1,0:T(8,128)S(1)} %mul.710, f32[16,18]{1,0:T(8,128)S(1)} %get-tuple-element.359, f32[13824,16]{0,1:T(8,128)S(1)} %fusion.72, f32[13824]{0:T(1024)S(1)} %get-tuple-element.324, f32[13824]{0:T(1024)S(1)} %get-tuple-element.325), kind=kOutput, calls=%fused_computation.3.clone.1 | convolution fusion | flops 48660480 | bytes 2876544 | tf_op jit(solution)/shard_map/while/body/eval_jaxpr/dot_general | solution.py:75
  212.5 1.2 convolution_add_fusion.2
  218.0 1.2 add_subtract_fusion.2
  222.8 1.3 dynamic-slice_reduce_fusion.5
  224.1 4.2 %convolution_multiply_fusion.3 = f32[13824,16]{0,1:T(8,128)S(1)} fusion(f32[18,13824]{1,0:T(8,128)S(1)} %mul.710, f32[16,18]{1,0:T(8,128)S(1)} %get-tuple-element.359, f32[13824,16]{0,1:T(8,128)S(1)} %fusion.72, f32[13824]{0:T(1024)S(1)} %get-tuple-element.324, f32[13824]{0:T(1024)S(1)} %get-tuple-element.325), kind=kOutput, calls=%fused_computation.3.clone.1 | convolution fusion | flops 48660480 | bytes 2876544 | tf_op jit(solution)/shard_map/while/body/eval_jaxpr/dot_general | solution.py:75
  228.3 1.2 convolution_add_fusion.2
  233.8 1.2 add_subtract_fusion.2
  238.6 1.3 dynamic-slice_reduce_fusion.5
  240.0 4.2 %convolution_multiply_fusion.3 = f32[13824,16]{0,1:T(8,128)S(1)} fusion(f32[18,13824]{1,0:T(8,128)S(1)} %mul.710, f32[16,18]{1,0:T(8,128)S(1)} %get-tuple-element.359, f32[13824,16]{0,1:T(8,128)S(1)} %fusion.72, f32[13824]{0:T(1024)S(1)} %get-tuple-element.324, f32[13824]{0:T(1024)S(1)} %get-tuple-element.325), kind=kOutput, calls=%fused_computation.3.clone.1 | convolution fusion | flops 48660480 | bytes 2876544 | tf_op jit(solution)/shard_map/while/body/eval_jaxpr/dot_general | solution.py:75
  249.6 1.2 add_subtract_fusion.2
  254.5 1.3 dynamic-slice_reduce_fusion.5
  255.8 4.2 %convolution_multiply_fusion.3 = f32[13824,16]{0,1:T(8,128)S(1)} fusion(f32[18,13824]{1,0:T(8,128)S(1)} %mul.710, f32[16,18]{1,0:T(8,128)S(1)} %get-tuple-element.359, f32[13824,16]{0,1:T(8,128)S(1)} %fusion.72, f32[13824]{0:T(1024)S(1)} %get-tuple-element.324, f32[13824]{0:T(1024)S(1)} %get-tuple-element.325), kind=kOutput, calls=%fused_computation.3.clone.1 | convolution fusion | flops 48660480 | bytes 2876544 | tf_op jit(solution)/shard_map/while/body/eval_jaxpr/dot_general | solution.py:75
  261.8 3.5 %all-to-all-start.3 = ((f32[8,16,3]{1,2,0:T(4,128)}), f32[8,16,3]{1,2,0:T(4,128)S(1)}, u32[]{:S(2)}, u32[]{:S(2)}) async-start(f32[8,16,3]{1,2,0:T(4,128)} %broadcast_in_dim.52), calls=%async_computation.3 | async-start | bytes 32768 | tf_op jit(solution)/shard_map/all_to_all | solution.py:36
  265.4 7.6 %all-to-all-done.3 = f32[8,16,3]{1,2,0:T(4,128)S(1)} async-done(((f32[8,16,3]{1,2,0:T(4,128)}), f32[8,16,3]{1,2,0:T(4,128)S(1)}, u32[]{:S(2)}, u32[]{:S(2)}) %all-to-all-start.3) | async-done | bytes 1568 | tf_op jit(solution)/shard_map/all_to_all | solution.py:36
  (175 shorter events, 69.3 us)
Async XLA Ops:
  0.6 102.6 %copy-start = (s32[512]{0:T(512)S(1)}, s32[512]{0:T(512)}, u32[]{:S(2)}) copy-start(s32[512]{0:T(512)} %param.15) | copy-start | bytes 6148
  3.0 12.5 %copy-start.5 = (s32[2,2]{1,0:T(2,128)S(1)}, s32[2,2]{1,0:T(2,128)}, u32[]{:S(2)}) copy-start(s32[2,2]{1,0:T(2,128)} %param.12) | copy-start | bytes 52
  15.6 8.0 %copy-start.1 = (bf16[2,2,2,256,1152]{3,2,4,1,0:T(2,128)(2,1)S(1)}, bf16[2,2,2,256,1152]{3,2,4,1,0:T(2,128)(2,1)}, u32[]{:S(2)}) copy-start(bf16[2,2,2,256,1152]{3,2,4,1,0:T(2,128)(2,1)} %copy.74) | copy-start | bytes 14155780
  46.5 1.8 copy-start.6
  51.9 52.4 %copy-start.3 = (f32[2,9,324]{2,0,1:T(2,128)S(1)}, f32[2,9,324]{2,0,1:T(2,128)}, u32[]{:S(2)}) copy-start(f32[2,9,324]{2,0,1:T(2,128)} %param.17) | copy-start | bytes 69988
  52.2 52.1 %copy-start.4 = (f32[3,512]{1,0:T(4,128)S(1)}, f32[3,512]{1,0:T(4,128)}, u32[]{:S(2)}) copy-start(f32[3,512]{1,0:T(4,128)} %param.16) | copy-start | bytes 18436
  52.3 74.5 %copy-start.7 = (f32[2]{0:T(128)S(1)}, f32[2]{0:T(128)}, u32[]{:S(2)}) copy-start(f32[2]{0:T(128)} %param.18) | copy-start | bytes 28
  59.2 59.2 %all-to-all-start.1 = ((f32[16,2,2,2,324]{4,3,2,1,0:T(2,128)}), f32[16,2,2,2,324]{4,3,2,1,0:T(2,128)S(1)}, u32[]{:S(2)}, u32[]{:S(2)}) async-start(f32[16,2,2,2,324]{4,3,2,1,0:T(2,128)} %bitcast.51), calls=%async_computation.1 | async-start | bytes 393216 | tf_op jit(solution)/shard_map/all_to_all | solution.py:24
  118.5 16.0 %copy-start.2 = (f32[2,2,2,324]{3,2,1,0:T(2,128)}, f32[2,2,2,324]{3,2,1,0:T(2,128)S(1)}, u32[]{:S(2)}) copy-start(f32[2,2,2,324]{3,2,1,0:T(2,128)S(1)} %reduce_sum.47) | copy-start | bytes 31108
  119.3 15.2 %all-to-all-start.2 = ((f32[8,2,18]{2,1,0:T(2,128)}), f32[8,2,18]{2,1,0:T(2,128)S(1)}, u32[]{:S(2)}, u32[]{:S(2)}) async-start(f32[8,2,18]{2,1,0:T(2,128)} %broadcast_in_dim.49), calls=%async_computation.2 | async-start | bytes 16384 | tf_op jit(solution)/shard_map/all_to_all | solution.py:36
  261.8 11.1 %all-to-all-start.3 = ((f32[8,16,3]{1,2,0:T(4,128)}), f32[8,16,3]{1,2,0:T(4,128)S(1)}, u32[]{:S(2)}, u32[]{:S(2)}) async-start(f32[8,16,3]{1,2,0:T(4,128)} %broadcast_in_dim.52), calls=%async_computation.3 | async-start | bytes 32768 | tf_op jit(solution)/shard_map/all_to_all | solution.py:36
where the time goes:
time: 275 us; the launch traced here: 274 us
  other arithmetic  63.4 us (23%)
  matrix products  61.5 us (22%)
  starting transfers between devices  54.7 us (20%)
  local copies, waits for them, and re-layouts  54.1 us (20%)
  waiting for transfers between devices  28.5 us (10%)
  loops' own time  6.53 us (2%)
  blocking collectives  4.07 us (1%)
    all_to_all x1, starting transfers between devices, sent_and_summed(): lax.all_to_all(tiles, axis, split_axis=0, concat_axis=0, tiled=True)  43.7 us
    dot_general x8, matrix products, force_block(): smooth = jnp.dot(moments, form_table, precision=highest)  33.5 us
    mul x32, other arithmetic, harmonics(): vectors.append(grid_step * signed.astype(jnp.float32))  23.7 us
    all_to_all x2, waiting for transfers between devices, from_everyone(): return lax.all_to_all(copies, axis, split_axis=0, concat_axis=0, tiled=True)  15.2 us
    unnamed x21, local copies, waits for them, and re-layouts  13.4 us
    all_to_all x1, waiting for transfers between devices, sent_and_summed(): lax.all_to_all(tiles, axis, split_axis=0, concat_axis=0, tiled=True)  13.3 us
    all_to_all x2, starting transfers between devices, from_everyone(): return lax.all_to_all(copies, axis, split_axis=0, concat_axis=0, tiled=True)  11 us
    slice x8, local copies, waits for them, and re-layouts, force_block(): pot_piece[0][None, :] * jnp.sin(phases)  10.4 us
  transfers between devices with their start and end apart: 3, of which 3 were waited for; matrix products, arithmetic and copies ran while one was open for 1% of the time, Pallas kernels for 0%

commit v1 on v0

v1 whole, which is shorter than its diff:
```python
import functools

import jax
import jax.numpy as jnp
import numpy as np
from jax import lax
from jax.experimental import pallas as pl
from jax.experimental.pallas import tpu as pltpu
from jax.sharding import PartitionSpec as P


NPROJ = 18
NL = 9
GRID = 96
LANES = 128
EDGE = 32
FOLD = 72
PACKED = NPROJ * NPROJ
WIDE = 384

grid_step = 0.0625

MONOMIALS = [
    (a, b, c) for a in range(4) for b in range(4) for c in range(4) if a + b + c <= 3
]
MONO_PAD = 32


def force_coefficients():
    shapes = [
        {(0, 0, 0): 1},
        {(1, 0, 0): 1},
        {(0, 1, 0): 1},
        {(0, 0, 1): 1},
        {(1, 1, 0): 1},
        {(0, 1, 1): 1},
        {(1, 0, 1): 1},
        {(2, 0, 0): 1, (0, 2, 0): -1},
        {(0, 0, 2): 2, (2, 0, 0): -1, (0, 2, 0): -1},
    ]
    table = np.zeros((16, LANES), np.float32)
    for l, terms in enumerate(shapes):
        for c in range(3):
            for powers, factor in terms.items():
                power = list(powers)
                power[c] += 1
                table[l, c * MONO_PAD + MONOMIALS.index(tuple(power))] += factor
    return table


def iota(shape, dim):
    return lax.broadcasted_iota(jnp.int32, shape, dim)


def div18(x):
    return (x * 3641) >> 16


def split(x):
    high = x.astype(jnp.bfloat16)
    return high, (x - high.astype(jnp.float32)).astype(jnp.bfloat16)


def dot_f32(a, b):
    return lax.dot_general(a, b, (((1,), (0,)), ((), ())), preferred_element_type=jnp.float32)


def gram_kernel(index, occ_ref, kw_ref, own_ref, x_ref, out_ref, xt_ref, acc_ref, y_ref):
    step = pl.program_id(0)
    spin, kpt = step // 2, step % 2
    bands, columns = x_ref.shape[3], x_ref.shape[4]
    tiles = columns // LANES
    kdim = 2 * bands

    @pl.when(step == 0)
    def _():
        acc_ref[...] = jnp.zeros_like(acc_ref)
        xt_ref[0:EDGE, :] = jnp.zeros((EDGE, kdim), jnp.bfloat16)
        xt_ref[EDGE + columns :, :] = jnp.zeros((EDGE, kdim), jnp.bfloat16)

    block, half, _ = index()
    count = occ_ref[spin, kpt] - half * bands
    mask = jnp.where(iota((bands, LANES), 0) < count, 1.0, 0.0).astype(jnp.bfloat16)
    weight = kw_ref[kpt]

    def turned(t):
        for c in range(2):
            block = x_ref[0, c, 0, :, t * LANES : (t + 1) * LANES]
            xt_ref[EDGE + t * LANES : EDGE + (t + 1) * LANES, c * bands : (c + 1) * bands] = block.T

    turned(0)
    for t in range(tiles):
        if t + 1 < tiles:
            turned(t + 1)
        real = x_ref[0, 0, 0, :, t * LANES : (t + 1) * LANES] * mask
        imag = x_ref[0, 1, 0, :, t * LANES : (t + 1) * LANES] * mask
        right = jnp.concatenate(
            [jnp.concatenate([real, imag], axis=1), jnp.concatenate([imag, -real], axis=1)], axis=0
        )
        left = xt_ref[t * LANES : (t + 1) * LANES + 2 * EDGE, :]
        gram = dot_f32(left, right)
        first = t * LANES - EDGE
        lane = iota((8, LANES), 1) + t * LANES
        rows = iota((8, LANES), 0)
        from_atom = rows - NPROJ * div18(lane)
        from_diagonal = rows - lane
        sums = [None] * (FOLD // 8)
        for v in range((LANES + 2 * EDGE) // 8):
            row = first + 8 * v
            if row < 0 or row >= columns:
                continue
            if row < t * LANES:
                value = gram[8 * v : 8 * v + 8, :LANES]
            elif row >= (t + 1) * LANES:
                value = gram[8 * v : 8 * v + 8, LANES:]
            else:
                value = jnp.where(
                    from_diagonal <= -row,
                    gram[8 * v : 8 * v + 8, :LANES],
                    gram[8 * v : 8 * v + 8, LANES:],
                )
            inside = (from_atom >= -row) & (from_atom < NPROJ - row)
            value = jnp.where(inside, value, 0.0)
            slot = (row // 8) % (FOLD // 8)
            sums[slot] = value if sums[slot] is None else sums[slot] + value
        for slot, value in enumerate(sums):
            acc_ref[spin, t, 8 * slot : 8 * slot + 8, :] += weight * value

    @pl.when(step == pl.num_programs(0) - 1)
    def _():
        own = own_ref[...]
        row = jnp.sum(jnp.where(iota(own.shape, 0) == block // 2, own, 0), axis=0, keepdims=True)
        row = jnp.where(block % 2 == 1, pltpu.roll(row, LANES // 2, 1), row)
        atoms = LANES // 2
        eye = iota((atoms, LANES), 0) == iota((atoms, LANES), 1)
        rowf = row.astype(jnp.float32)
        col = jnp.sum(jnp.where(eye, rowf, 0.0), axis=1, keepdims=True)
        earlier = (col == rowf) & (iota((atoms, LANES), 0) < iota((atoms, LANES), 1))
        slot = jnp.sum(jnp.where(earlier, 1.0, 0.0), axis=0, keepdims=True)
        place = rowf * 4.0 + slot
        place = jnp.where(iota((1, LANES), 1) < atoms, place, pltpu.roll(place, atoms, 1))
        out_row = iota((LANES, LANES), 0).astype(jnp.float32)
        picks = [
            jnp.where(place + 2.0 * s == out_row, 1.0, 0.0).astype(jnp.bfloat16) for s in range(2)
        ]
        pick = jnp.concatenate(picks, axis=1)
        parts = []
        for s in range(2):
            for t in range(tiles):
                folded = acc_ref[s, t, 0:24, :]
                for q in range(1, FOLD // NPROJ):
                    folded = folded + acc_ref[s, t, NPROJ * q : NPROJ * q + 24, :]
                padded = jnp.concatenate(
                    [folded, jnp.zeros((LANES - 24, LANES), jnp.float32)], axis=0
                )
                y_ref[t * LANES : (t + 1) * LANES, :] = padded.T
            lane = iota((atoms, LANES), 1)
            packed = [jnp.zeros((atoms, LANES), jnp.float32) for _ in range(WIDE // LANES)]
            for j in range(NPROJ):
                piece = y_ref[pl.ds(j, atoms, stride=NPROJ), :]
                start = NPROJ * j
                shift = start % LANES
                if shift:
                    piece = pltpu.roll(piece, shift, 1)
                tile = start // LANES
                here = (lane >= shift) & (lane < shift + NPROJ)
                packed[tile] = jnp.where(here, piece, packed[tile])
                if shift + NPROJ > LANES:
                    packed[tile + 1] = jnp.where(
                        lane < shift + NPROJ - LANES, piece, packed[tile + 1]
                    )
            high, low = split(jnp.concatenate(packed, axis=1))
            parts += [high, low]
        result = dot_f32(pick, jnp.concatenate(parts, axis=0))
        for owner in range(out_ref.shape[0]):
            out_ref[owner] = result[4 * owner : 4 * owner + 4]


def gram(index, occupied, kweights, owners, coefficients, interpret=False):
    spins, comps, kpts, bands, columns = coefficients.shape
    tiles = columns // LANES
    smem = pl.BlockSpec(memory_space=pltpu.SMEM)
    return pl.pallas_call(
        functools.partial(gram_kernel, index),
        grid=(spins * kpts,),
        in_specs=[
            smem,
            smem,
            pl.BlockSpec((4, LANES), lambda g: (0, 0)),
            pl.BlockSpec((1, comps, 1, bands, columns), lambda g: (g // 2, 0, g % 2, 0, 0)),
        ],
        out_specs=pl.BlockSpec((LANES // 4, 4, WIDE), lambda g: (0, 0, 0)),
        out_shape=jax.ShapeDtypeStruct((LANES // 4, 4, WIDE), jnp.float32),
        scratch_shapes=[
            pltpu.VMEM((columns + 2 * EDGE, comps * bands), jnp.bfloat16),
            pltpu.VMEM((spins, tiles, 80, LANES), jnp.float32),
            pltpu.VMEM((columns, LANES), jnp.float32),
        ],
        cost_estimate=pl.CostEstimate(
            flops=2 * spins * kpts * columns * 192 * 2 * 2 * bands,
            bytes_accessed=spins * comps * kpts * bands * columns * 2,
            transcendentals=0,
        ),
        name="gram",
        interpret=interpret,
    )(occupied, kweights, owners, coefficients)


def sin_turns(t):
    t = t - jnp.floor(t + 0.5)
    t = jnp.where(t > 0.25, 0.5 - t, jnp.where(t < -0.25, -0.5 - t, t))
    x = t * np.float32(2.0 * np.pi)
    x2 = x * x
    p = np.float32(-1.0 / 39916800.0)
    for c in (1.0 / 362880.0, -1.0 / 5040.0, 1.0 / 120.0, -1.0 / 6.0):
        p = p * x2 + np.float32(c)
    return x + x * x2 * p


def signed(index):
    return jnp.where(index >= GRID // 2, index - GRID, index).astype(jnp.float32)


def wave_kernel(index, widths_ref, own_ref, species_ref, pos_ref, pot_ref, out_ref, kinds_ref, uh_ref, ul_ref):
    lines = 4
    rows = pot_ref.shape[0] // 6
    planes = rows * lines // GRID
    group = GRID // lines
    block, _, mine = index()
    own = own_ref[...]
    atoms = 16

    def spread(a):
        return jnp.concatenate([jnp.broadcast_to(a[r : r + 1], (4, LANES)) for r in range(4)], axis=0)

    at, lane16 = iota((atoms, LANES), 0), iota((atoms, LANES), 1)
    hit = (spread(own) == mine) & (lane16 // 64 == (at // 2) % 2)
    lanef = lane16.astype(jnp.float32)
    low = jnp.min(jnp.where(hit, lanef, 1e9), axis=1, keepdims=True)
    high = jnp.max(jnp.where(hit, lanef, -1.0), axis=1, keepdims=True)
    chosen = lanef == jnp.where(at % 2 == 1, high, low)

    lane = iota((1, LANES), 1)
    alpha, imag = (lane // atoms) % 4, lane // 64

    def on_lanes(a):
        column = jnp.sum(jnp.where(chosen, a, 0.0), axis=1, keepdims=True)
        return jnp.sum(jnp.where(at == lane16 % atoms, column, 0.0), axis=0, keepdims=True)

    place = [
        on_lanes(
            jnp.concatenate(
                [
                    jnp.broadcast_to(pos_ref[c : c + 1, r * LANES : (r + 1) * LANES], (4, LANES))
                    for r in range(4)
                ],
                axis=0,
            )
        )
        for c in range(3)
    ]
    kind = on_lanes(spread(species_ref[...]).astype(jnp.float32))
    width = jnp.where(kind > 0.5, widths_ref[1], widths_ref[0])
    turns = [p * np.float32(grid_step / (2.0 * np.pi)) for p in place]

    def power(g, exponent):
        g2 = g * g
        return jnp.where(
            exponent == 0, 1.0, jnp.where(exponent == 1, g, jnp.where(exponent == 2, g2, g2 * g))
        )

    mx = signed(iota((GRID, LANES), 0))
    gx = mx * grid_step
    phase = mx * turns[0]
    phase = phase - jnp.floor(phase + 0.5)
    factor = jnp.exp(-width * (gx * gx)) * power(gx, alpha)
    uh_ref[...] = jnp.zeros_like(uh_ref)
    ul_ref[...] = jnp.zeros_like(ul_ref)
    for c in range(2):
        shift = jnp.where(imag == 0, 0.25 + 0.25 * c, 0.25 * c)
        h, l = split(sin_turns(phase + shift) * factor)
        for line in range(lines):
            r = c * WIDE + line * GRID
            uh_ref[r : r + GRID, line * LANES : (line + 1) * LANES] = h
            ul_ref[r : r + GRID, line * LANES : (line + 1) * LANES] = l

    pieces = [
        split(pot_ref[pl.ds(2 * k + c, rows, stride=6), :]) for c in range(2) for k in range(3)
    ]
    vh = jnp.concatenate([p[0] for p in pieces], axis=1)
    vl = jnp.concatenate([p[1] for p in pieces], axis=1)
    first = dot_f32(vh, uh_ref[...]) + dot_f32(vl, uh_ref[...]) + dot_f32(vh, ul_ref[...])

    def tiled(a):
        return jnp.concatenate([a] * lines, axis=1)

    my = signed(lines * iota((group, lines * LANES), 0) + iota((group, lines * LANES), 1) // LANES)
    gy = my * grid_step
    phase = my * tiled(turns[1])
    phase = phase - jnp.floor(phase + 0.5)
    shift = tiled(jnp.where(imag == 0, 0.0, 0.25))
    damp = jnp.exp(-tiled(width) * (gy * gy))
    y1 = sin_turns(phase + shift) * damp
    y2 = sin_turns(phase + shift + 0.25) * damp

    zi = iota((16, LANES), 0) + block * planes
    mz = signed(jnp.where(zi >= GRID, zi - GRID, zi))
    gz = mz * grid_step
    phase = mz * turns[2]
    phase = phase - jnp.floor(phase + 0.5)
    damp = jnp.exp(-width * (gz * gz))
    zs = sin_turns(phase) * damp
    zc = sin_turns(phase + 0.25) * damp

    sums = {}
    for z in range(planes):
        wave = y1 * tiled(zc[z : z + 1]) + y2 * tiled(zs[z : z + 1])
        term = first[z * group : (z + 1) * group] * wave
        gz_row = gz[z : z + 1]
        for b in range(4):
            if b:
                term = term * gy
            total = None
            for r in range(0, group, 8):
                for line in range(lines):
                    piece = term[r : r + 8, line * LANES : (line + 1) * LANES]
                    total = piece if total is None else total + piece
            for c in range(4 - b):
                if c:
                    total = total * gz_row
                sums[b, c] = total if z == 0 else sums[b, c] + total
    reduced = {k: jnp.sum(v, axis=0, keepdims=True) for k, v in sums.items()}
    which = iota((MONO_PAD, LANES), 0)
    table = jnp.zeros((MONO_PAD, LANES), jnp.float32)
    for m, (a, b, c) in enumerate(MONOMIALS):
        table = jnp.where((which == m) & (alpha == a), reduced[b, c], table)
    aux = jnp.where(which == 0, kind, 0.0)
    turned = jnp.concatenate([table, aux, jnp.zeros((64, LANES), jnp.float32)], axis=0).T
    result = turned[0:atoms]
    for g in range(1, LANES // atoms):
        result = result + turned[g * atoms : (g + 1) * atoms]
    lane = iota((atoms, LANES), 1)
    sent = jnp.where(lane < MONO_PAD, result, 0.0)
    kinds_ref[...] = result
    for row in range(4):
        line = sent[4 * row : 4 * row + 1]
        for k in range(1, 4):
            line = line + pltpu.roll(sent[4 * row + k : 4 * row + k + 1], MONO_PAD * k, 1)
        out_ref[row : row + 1, :] = line


def waves(index, widths, owners, species, positions, potential, interpret=False):
    smem = pl.BlockSpec(memory_space=pltpu.SMEM)
    vmem = pl.BlockSpec(memory_space=pltpu.VMEM)
    return pl.pallas_call(
        functools.partial(wave_kernel, index),
        in_specs=[smem, vmem, vmem, vmem, vmem],
        out_specs=(vmem, vmem),
        out_shape=(
            jax.ShapeDtypeStruct((4, LANES), jnp.float32),
            jax.ShapeDtypeStruct((16, LANES), jnp.float32),
        ),
        scratch_shapes=[pltpu.VMEM((2 * WIDE, 4 * LANES), jnp.bfloat16)] * 2,
        cost_estimate=pl.CostEstimate(
            flops=2 * 288 * 768 * 512 * 3, bytes_accessed=potential.size * 4, transcendentals=0
        ),
        compiler_params=pltpu.CompilerParams(vmem_limit_bytes=16 << 20),
        name="waves",
        interpret=interpret,
    )(widths, owners, species, positions, potential)


def final_kernel(index, parts_ref, sums_ref, kinds_ref, mult_ref, coef_ref, density_ref, forces_ref):
    total = parts_ref[0]
    for r in range(1, parts_ref.shape[0]):
        total = total + parts_ref[r]
    z = jnp.concatenate([total, total], axis=0)
    r = iota((WIDE, WIDE), 0)
    u = div18(r)
    swap = (iota((WIDE, WIDE), 1) == (r - NPROJ * u) * NPROJ + u) & (r < PACKED)
    swap = jnp.where(swap, 1.0, 0.0).astype(jnp.bfloat16)
    high = z.astype(jnp.bfloat16)
    rest = z - high.astype(jnp.float32)
    middle = rest.astype(jnp.bfloat16)
    low = (rest - middle.astype(jnp.float32)).astype(jnp.bfloat16)
    turned = dot_f32(high, swap) + dot_f32(middle, swap) + dot_f32(low, swap)
    e = iota((8, WIDE), 1)
    u = div18(e)
    v = e - NPROJ * u
    real = jnp.where(v <= u, z, turned)
    imag = jnp.where(u > v, turned, jnp.where(u < v, -z, 0.0))
    for s in range(2):
        density_ref[s, 0] = real[2 * s : 2 * s + 2, :PACKED]
        density_ref[s, 1] = imag[2 * s : 2 * s + 2, :PACKED]

    both = real + pltpu.roll(real, 2, 0)
    block = index()[0]
    line = jnp.broadcast_to(sums_ref[pl.ds(block // 2, 1), :], (8, LANES))
    lane, row = iota((8, LANES), 1), iota((8, LANES), 0)
    line = jnp.where(block % 2 == 1, pltpu.roll(line, 2 * MONO_PAD, 1), line)
    line = jnp.where(row % 2 == 1, pltpu.roll(line, 3 * MONO_PAD, 1), line)
    line = jnp.where(lane < MONO_PAD, line, 0.0)
    sums = line + pltpu.roll(line, MONO_PAD, 1) + pltpu.roll(line, 2 * MONO_PAD, 1)
    kinds = jnp.concatenate([kinds_ref[pl.ds(2 * block, 2), :]] * 4, axis=0)
    kind = jnp.sum(jnp.where(lane == MONO_PAD, kinds, 0.0), axis=1, keepdims=True) > 4.0
    poly = jnp.zeros((8, LANES), jnp.float32)
    for l in range(NL):
        chosen = jnp.where(kind, mult_ref[l, 1:2, :], mult_ref[l, 0:1, :])
        moment = jnp.sum(both[:, :PACKED] * chosen, axis=1, keepdims=True)
        poly = poly + moment * coef_ref[l : l + 1, :]
    terms = poly * sums
    forces = jnp.concatenate(
        [
            jnp.sum(jnp.where(lane // MONO_PAD == c, terms, 0.0), axis=1, keepdims=True)
            for c in range(3)
        ],
        axis=1,
    )
    forces_ref[...] = forces[0:2, :]


def final(index, parts, sums, kinds, multipole, coefs, interpret=False):
    vmem = pl.BlockSpec(memory_space=pltpu.VMEM)
    return pl.pallas_call(
        functools.partial(final_kernel, index),
        in_specs=[vmem] * 5,
        out_specs=(vmem, vmem),
        out_shape=(
            jax.ShapeDtypeStruct((2, 2, 2, PACKED), jnp.float32),
            jax.ShapeDtypeStruct((2, 3), jnp.float32),
        ),
        cost_estimate=pl.CostEstimate(flops=10**7, bytes_accessed=10**5, transcendentals=0),
        compiler_params=pltpu.CompilerParams(vmem_limit_bytes=8 << 20),
        name="final",
        interpret=interpret,
    )(parts, sums, kinds, multipole, coefs)


def place():
    half = lax.axis_index("ba")
    return lax.axis_index("ga"), half, lax.axis_index("ka") * lax.axis_size("ba") + half


def step(
    coefficients, occupied, kweights, owner_map, species, positions, multipole, widths, potential
):
    owners = owner_map.reshape(4, LANES)
    packed = gram(place, occupied, kweights, owners, coefficients)
    packed, widths, positions, species, potential, multipole = lax.optimization_barrier(
        (packed, widths, positions, species, potential, multipole)
    )
    arrived = lax.all_to_all(packed, ("ka", "ba"), split_axis=0, concat_axis=0, tiled=True)
    values = potential.reshape(2, -1, LANES).transpose(1, 0, 2).reshape(-1, LANES)
    sums, kinds = waves(place, widths, owners, species.reshape(4, LANES), positions, values)
    sums = lax.psum(sums, "ga")
    density, forces = final(
        place, arrived, sums, kinds, multipole.transpose(1, 0, 2), jnp.asarray(force_coefficients())
    )
    return density, forces.T


def solution(mesh):
    placed = (
        P(None, None, ("grp", "ka"), "ba", "ga"),
        P(None, ("grp", "ka")),
        P(("grp", "ka")),
        P("grp"),
        P("grp"),
        P(None, "grp"),
        P(),
        P(),
        P(None, ("grp", "ga")),
    )
    return jax.shard_map(
        step,
        mesh=mesh,
        in_specs=placed,
        out_specs=(
            P(None, None, ("grp", "ka", "ga", "ba"), None),
            P(None, ("grp", "ka", "ga", "ba")),
        ),
        check_vma=False,
    )
```

time: 275 us -> 73.2 us (0.27)
  other arithmetic: 63.4 us -> 0 us
  matrix products: 61.5 us -> 0 us
  local copies, waits for them, and re-layouts: 54.1 us -> 0.03 us
  waiting for transfers between devices: 28.5 us -> 0.01 us
  blocking collectives: 4.07 us -> 18 us
  starting transfers between devices: 54.7 us -> 44.4 us
  Pallas kernels: 0 us -> 9.76 us
  loops' own time: 6.53 us -> 0 us
    dot_general x27 -> x0, matrix products: 61.5 us -> none  [the longest x8 33.5 us: force_block(): smooth = jnp.dot(moments, form_table, precision=highest)]
    mul x50 -> x0, other arithmetic: 41.6 us -> none  [the longest x32 23.7 us: harmonics(): vectors.append(grid_step * signed.astype(jnp.float32))]
    all_to_all x3 -> x1, waiting for transfers between devices: 28.5 us -> 0.01 us  [step(): lax.all_to_all(packed, ('ka', 'ba'), split_axis=0, concat_axis=0, tiled=T...]
    psum x0 -> x1, blocking collectives: none -> 18 us  [step(): sums = lax.psum(sums, 'ga')]
    unnamed x21 -> x14, local copies, waits for them, and re-layouts: 13.4 us -> 0.03 us
    another operation x18 -> x0, local copies, waits for them, and re-layouts: 11.8 us -> none  [the longest x8 6.75 us: harmonics(): jnp.stack([jnp.ones_like(square), along_x, along_y, along_z, along_x * al...]
    slice x8 -> x0, local copies, waits for them, and re-layouts: 10.4 us -> none  [force_block(): pot_piece[0][None, :] * jnp.sin(phases)]
    all_to_all x3 -> x1, starting transfers between devices: 54.7 us -> 44.4 us  [step(): lax.all_to_all(packed, ('ka', 'ba'), split_axis=0, concat_axis=0, tiled=T...]
  transfers between devices with their start and end apart: 3 -> 1, of which waited for: 3 -> 0; matrix products, arithmetic and copies ran while one was open for 1% -> 0% of each run, Pallas kernels for 0% -> 3%
where the time goes in v1:
time: 73.2 us; the launch traced here: 73 us
  starting transfers between devices  44.4 us (61%)
  blocking collectives  18 us (25%)
  Pallas kernels  9.76 us (13%)
  between operations  0.75 us (1%)
    all_to_all x1, starting transfers between devices, step(): lax.all_to_all(packed, ('ka', 'ba'), split_axis=0, concat_axis=0, tiled=T...  44.4 us
    psum x1, blocking collectives, step(): sums = lax.psum(sums, 'ga')  18 us
    pallas_call x1, Pallas kernels, gram(): pl.pallas_call(functools.partial(gram_kernel, index), grid=(spins * kpts,...  6.71 us
    pallas_call x1, Pallas kernels, waves(): pl.pallas_call(functools.partial(wave_kernel, index), in_specs=[smem, vme...  2.01 us
  transfers between devices with their start and end apart: 1, of which 0 were waited for; matrix products, arithmetic and copies ran while one was open for 0% of the time, Pallas kernels for 3%

profile of v1, /device:TPU:80, one launch (start us, length us, event | category | flops | bytes accessed | tf_op | source)
XLA Modules:
  0.0 73.0 jit_solution(15487087480519417732)
XLA Ops:
  0.6 0.0 copy-start.4
  0.6 0.0 copy-start.2
  0.7 0.0 copy-start.6
  0.7 0.0 copy-start.3
  0.7 0.0 copy-start.5
  0.7 0.0 copy-start
  0.7 0.0 copy-start.1
  0.7 6.7 %gram.1 = f32[32,4,384]{2,1,0:T(4,128)} custom-call(s32[2,2]{1,0:T(2,128)} %occ_ref.1, f32[2]{0:T(128)} %kw_ref.1, s32[4,128]{1,0:T(4,128)} %bitcast.11, bf16[2,2,2,256,1152]{4,3,2,1,0:T(8,128)(2,1)} %x_ref.1), custom_call_target="tpu_custom_call" | custom-call | flops 1811939328 | bytes 4718592 | tf_op jit(solution)/shard_map/gram/pallas_call | solution.py:183
  7.4 44.4 %all-to-all-start = ((f32[32,4,384]{2,1,0:T(4,128)}), f32[32,4,384]{2,1,0:T(4,128)S(1)}, u32[]{:S(2)}, u32[]{:S(2)}) async-start(f32[32,4,384]{2,1,0:T(4,128)} %gram.1), calls=%async_computation | async-start | bytes 393216 | tf_op jit(solution)/shard_map/all_to_all | solution.py:452
  51.9 0.0 copy-done.4
  51.9 0.0 copy-done.2
  51.9 0.0 copy-done.6
  51.9 0.0 copy-done.3
  51.9 0.0 copy-done.5
  51.9 2.0 %waves.1 = (f32[4,128]{1,0:T(4,128)S(1)}, f32[16,128]{1,0:T(8,128)S(1)}) custom-call(f32[2]{0:T(128)S(1)} %copy-done.6, s32[4,128]{1,0:T(4,128)S(1)} %bitcast.12, s32[4,128]{1,0:T(4,128)S(1)} %bitcast.13, f32[3,512]{1,0:T(4,128)S(1)} %copy-done.3, f32[1728,128]{1,0:T(8,128)S(1)} %bitcast.10), custom_call_target="tpu_custom_call" | custom-call | flops 679477248 | bytes 884736 | tf_op jit(solution)/shard_map/waves/pallas_call | solution.py:355
  53.9 18.0 %psum.7.sums_ref = f32[4,128]{1,0:T(4,128)S(1)} all-reduce(f32[4,128]{1,0:T(4,128)S(1)} %get-tuple-element.17), channel_id=1, replica_groups=mesh['grp'=2,'ka'=16,'ga'=8,'ba'=2] {'ga'}, use_global_device_ids=true, to_apply=%region_0.0 | all-reduce | flops 512 | bytes 4096 | tf_op jit(solution)/shard_map/psum | solution.py:455
  71.9 0.0 all-to-all-done.parts_ref
  71.9 0.0 copy-done
  71.9 0.0 copy-done.1
  72.0 1.0 %final.1 = (f32[2,2,2,324]{3,2,1,0:T(2,128)}, f32[2,3]{1,0:T(2,128)}) custom-call(f32[32,4,384]{2,1,0:T(4,128)S(1)} %all-to-all-done.parts_ref, f32[4,128]{1,0:T(4,128)S(1)} %psum.7.sums_ref, f32[16,128]{1,0:T(8,128)S(1)} %get-tuple-element.18.kinds_ref, f32[9,2,324]{2,1,0:T(2,128)S(1)} %bitcast.9, f32[16,128]{1,0:T(8,128)S(1)} %copy-done.1), custom_call_target="tpu_custom_call" | custom-call | flops 10000000 | bytes 100000 | tf_op jit(solution)/shard_map/final/pallas_call | solution.py:424
Async XLA Ops:
  0.6 51.2 %copy-start.4 = (s32[512]{0:T(512)S(1)}, s32[512]{0:T(512)}, u32[]{:S(2)}) copy-start(s32[512]{0:T(512)} %param.13) | copy-start | bytes 6148
  0.6 51.2 %copy-start.2 = (f32[2,110592]{1,0:T(2,128)S(1)}, f32[2,110592]{1,0:T(2,128)}, u32[]{:S(2)}) copy-start(f32[2,110592]{1,0:T(2,128)} %param.18) | copy-start | bytes 2654212
  0.7 51.2 %copy-start.6 = (f32[2]{0:T(128)S(1)}, f32[2]{0:T(128)}, u32[]{:S(2)}) copy-start(f32[2]{0:T(128)} %widths_ref) | copy-start | bytes 28
  0.7 51.2 %copy-start.3 = (f32[3,512]{1,0:T(4,128)S(1)}, f32[3,512]{1,0:T(4,128)}, u32[]{:S(2)}) copy-start(f32[3,512]{1,0:T(4,128)} %pos_ref) | copy-start | bytes 18436
  0.7 51.2 %copy-start.5 = (s32[512]{0:T(512)S(1)}, s32[512]{0:T(512)}, u32[]{:S(2)}) copy-start(s32[512]{0:T(512)} %param.14) | copy-start | bytes 6148
  0.7 71.3 %copy-start = (f32[2,9,324]{2,0,1:T(2,128)S(1)}, f32[2,9,324]{2,0,1:T(2,128)}, u32[]{:S(2)}) copy-start(f32[2,9,324]{2,0,1:T(2,128)} %param.16) | copy-start | bytes 69988
  0.7 71.3 %copy-start.1 = (f32[16,128]{1,0:T(8,128)S(1)}, f32[16,128]{1,0:T(8,128)}, u32[]{:S(2)}) copy-start(f32[16,128]{1,0:T(8,128)} %constant.2.clone.coef_ref) | copy-start | bytes 24580
  7.4 64.5 %all-to-all-start = ((f32[32,4,384]{2,1,0:T(4,128)}), f32[32,4,384]{2,1,0:T(4,128)S(1)}, u32[]{:S(2)}, u32[]{:S(2)}) async-start(f32[32,4,384]{2,1,0:T(4,128)} %gram.1), calls=%async_computation | async-start | bytes 393216 | tf_op jit(solution)/shard_map/all_to_all | solution.py:452

commit v2 on v1

--- a/solution.py
+++ b/solution.py
@@ -13,7 +13,7 @@
 NL = 9
 GRID = 96
 LANES = 128
-EDGE = 32
+EDGE = 16
 FOLD = 72
 PACKED = NPROJ * NPROJ
 WIDE = 384
@@ -24,6 +24,8 @@
     (a, b, c) for a in range(4) for b in range(4) for c in range(4) if a + b + c <= 3
 ]
 MONO_PAD = 32
+GRAM_VMEM = 60 << 20
+FIRST = 4
 
 
 def force_coefficients():
@@ -65,139 +67,194 @@
     return lax.dot_general(a, b, (((1,), (0,)), ((), ())), preferred_element_type=jnp.float32)
 
 
-def gram_kernel(index, occ_ref, kw_ref, own_ref, x_ref, out_ref, xt_ref, acc_ref, y_ref):
-    step = pl.program_id(0)
-    spin, kpt = step // 2, step % 2
-    bands, columns = x_ref.shape[3], x_ref.shape[4]
+def gram_kernel(
+    index, occ_hbm, kw_hbm, own_hbm, x_hbm, out_ref,
+    occ_ref, kw_ref, own_ref, x_ref, xt_ref, acc_ref, y_ref, parts_ref, sems, small_sems,
+):
+    spins, comps, kpts, bands, columns = x_hbm.shape
     tiles = columns // LANES
-    kdim = 2 * bands
-
-    @pl.when(step == 0)
-    def _():
-        acc_ref[...] = jnp.zeros_like(acc_ref)
-        xt_ref[0:EDGE, :] = jnp.zeros((EDGE, kdim), jnp.bfloat16)
-        xt_ref[EDGE + columns :, :] = jnp.zeros((EDGE, kdim), jnp.bfloat16)
-
     block, half, _ = index()
-    count = occ_ref[spin, kpt] - half * bands
-    mask = jnp.where(iota((bands, LANES), 0) < count, 1.0, 0.0).astype(jnp.bfloat16)
-    weight = kw_ref[kpt]
-
-    def turned(t):
-        for c in range(2):
-            block = x_ref[0, c, 0, :, t * LANES : (t + 1) * LANES]
-            xt_ref[EDGE + t * LANES : EDGE + (t + 1) * LANES, c * bands : (c + 1) * bands] = block.T
-
-    turned(0)
-    for t in range(tiles):
-        if t + 1 < tiles:
-            turned(t + 1)
-        real = x_ref[0, 0, 0, :, t * LANES : (t + 1) * LANES] * mask
-        imag = x_ref[0, 1, 0, :, t * LANES : (t + 1) * LANES] * mask
-        right = jnp.concatenate(
-            [jnp.concatenate([real, imag], axis=1), jnp.concatenate([imag, -real], axis=1)], axis=0
+
+    cuts = [(0, 0, FIRST), (0, FIRST, tiles), (1, 0, tiles)]
+
+    def arrivals(n):
+        s, low, high = cuts[n]
+        part = pl.ds(low * LANES, (high - low) * LANES)
+        return [
+            pltpu.make_async_copy(
+                x_hbm.at[s, c, k, :, part], x_ref.at[s, c, k, :, part], sems.at[n, c, k]
+            )
+            for k in range(kpts)
+            for c in range(comps)
+        ]
+
+    small = [
+        pltpu.make_async_copy(src, dst, small_sems.at[n])
+        for n, (src, dst) in enumerate(
+            ((occ_hbm, occ_ref), (kw_hbm, kw_ref), (own_hbm, own_ref))
         )
-        left = xt_ref[t * LANES : (t + 1) * LANES + 2 * EDGE, :]
-        gram = dot_f32(left, right)
-        first = t * LANES - EDGE
-        lane = iota((8, LANES), 1) + t * LANES
-        rows = iota((8, LANES), 0)
-        from_atom = rows - NPROJ * div18(lane)
-        from_diagonal = rows - lane
-        sums = [None] * (FOLD // 8)
-        for v in range((LANES + 2 * EDGE) // 8):
-            row = first + 8 * v
-            if row < 0 or row >= columns:
-                continue
-            if row < t * LANES:
-                value = gram[8 * v : 8 * v + 8, :LANES]
-            elif row >= (t + 1) * LANES:
-                value = gram[8 * v : 8 * v + 8, LANES:]
-            else:
-                value = jnp.where(
-                    from_diagonal <= -row,
-                    gram[8 * v : 8 * v + 8, :LANES],
-                    gram[8 * v : 8 * v + 8, LANES:],
+    ]
+    for copy in small:
+        copy.start()
+    for n in range(2):
+        for copy in arrivals(n):
+            copy.start()
+
+    acc_ref[:, FOLD:, :] = jnp.zeros((tiles, 80 - FOLD, LANES), jnp.float32)
+    edge = jnp.zeros((kpts, EDGE, comps * bands), jnp.bfloat16)
+    xt_ref[:, 0:EDGE, :] = edge
+    xt_ref[:, EDGE + columns :, :] = edge
+    for copy in small:
+        copy.wait()
+    atoms = LANES // 2
+
+    def spin_part(s):
+        band = iota((1, comps * bands), 1) % bands
+        masks = [
+            jnp.where(band < occ_ref[s, k] - half * bands, 1.0, 0.0).astype(jnp.bfloat16)
+            for k in range(kpts)
+        ]
+
+        def turned(t):
+            for k in range(kpts):
+                block_t = jnp.concatenate(
+                    [x_ref[s, c, k, :, t * LANES : (t + 1) * LANES].T for c in range(comps)],
+                    axis=1,
                 )
-            inside = (from_atom >= -row) & (from_atom < NPROJ - row)
-            value = jnp.where(inside, value, 0.0)
-            slot = (row // 8) % (FOLD // 8)
-            sums[slot] = value if sums[slot] is None else sums[slot] + value
-        for slot, value in enumerate(sums):
-            acc_ref[spin, t, 8 * slot : 8 * slot + 8, :] += weight * value
-
-    @pl.when(step == pl.num_programs(0) - 1)
-    def _():
-        own = own_ref[...]
-        row = jnp.sum(jnp.where(iota(own.shape, 0) == block // 2, own, 0), axis=0, keepdims=True)
-        row = jnp.where(block % 2 == 1, pltpu.roll(row, LANES // 2, 1), row)
-        atoms = LANES // 2
-        eye = iota((atoms, LANES), 0) == iota((atoms, LANES), 1)
-        rowf = row.astype(jnp.float32)
-        col = jnp.sum(jnp.where(eye, rowf, 0.0), axis=1, keepdims=True)
-        earlier = (col == rowf) & (iota((atoms, LANES), 0) < iota((atoms, LANES), 1))
-        slot = jnp.sum(jnp.where(earlier, 1.0, 0.0), axis=0, keepdims=True)
-        place = rowf * 4.0 + slot
-        place = jnp.where(iota((1, LANES), 1) < atoms, place, pltpu.roll(place, atoms, 1))
-        out_row = iota((LANES, LANES), 0).astype(jnp.float32)
-        picks = [
-            jnp.where(place + 2.0 * s == out_row, 1.0, 0.0).astype(jnp.bfloat16) for s in range(2)
-        ]
-        pick = jnp.concatenate(picks, axis=1)
-        parts = []
-        for s in range(2):
-            for t in range(tiles):
-                folded = acc_ref[s, t, 0:24, :]
-                for q in range(1, FOLD // NPROJ):
-                    folded = folded + acc_ref[s, t, NPROJ * q : NPROJ * q + 24, :]
-                padded = jnp.concatenate(
-                    [folded, jnp.zeros((LANES - 24, LANES), jnp.float32)], axis=0
+                xt_ref[k, EDGE + t * LANES : EDGE + (t + 1) * LANES, :] = block_t * masks[k]
+
+        def arrived(t):
+            for n, cut in enumerate(cuts):
+                if cut[:2] == (s, t):
+                    for copy in arrivals(n):
+                        copy.wait()
+                    if n == 0:
+                        for copy in arrivals(2):
+                            copy.start()
+
+        arrived(0)
+        turned(0)
+        for t in range(tiles):
+            if t + 1 < tiles:
+                arrived(t + 1)
+                turned(t + 1)
+            lane = iota((8, LANES), 1) + t * LANES
+            rows = iota((8, LANES), 0)
+            from_atom = rows - NPROJ * div18(lane)
+            from_diagonal = rows - lane
+            grams = []
+            for k in range(kpts):
+                real = x_ref[s, 0, k, :, t * LANES : (t + 1) * LANES]
+                imag = x_ref[s, 1, k, :, t * LANES : (t + 1) * LANES]
+                right = jnp.concatenate(
+                    [
+                        jnp.concatenate([real, imag], axis=1),
+                        jnp.concatenate([imag, -real], axis=1),
+                    ],
+                    axis=0,
                 )
-                y_ref[t * LANES : (t + 1) * LANES, :] = padded.T
-            lane = iota((atoms, LANES), 1)
-            packed = [jnp.zeros((atoms, LANES), jnp.float32) for _ in range(WIDE // LANES)]
-            for j in range(NPROJ):
-                piece = y_ref[pl.ds(j, atoms, stride=NPROJ), :]
-                start = NPROJ * j
-                shift = start % LANES
-                if shift:
-                    piece = pltpu.roll(piece, shift, 1)
-                tile = start // LANES
-                here = (lane >= shift) & (lane < shift + NPROJ)
-                packed[tile] = jnp.where(here, piece, packed[tile])
-                if shift + NPROJ > LANES:
-                    packed[tile + 1] = jnp.where(
-                        lane < shift + NPROJ - LANES, piece, packed[tile + 1]
-                    )
-            high, low = split(jnp.concatenate(packed, axis=1))
-            parts += [high, low]
-        result = dot_f32(pick, jnp.concatenate(parts, axis=0))
-        for owner in range(out_ref.shape[0]):
-            out_ref[owner] = result[4 * owner : 4 * owner + 4]
+                left = xt_ref[k, t * LANES : (t + 1) * LANES + 2 * EDGE, :]
+                grams.append(dot_f32(left, right))
+            first = t * LANES - EDGE
+            sums = [None] * (FOLD // 8)
+            for v in range((LANES + 2 * EDGE) // 8):
+                row = first + 8 * v
+                if row < 0 or row >= columns:
+                    continue
+                if row + 8 <= NPROJ * (t * LANES // NPROJ):
+                    continue
+                if row >= NPROJ * -(-(t + 1) * LANES // NPROJ):
+                    continue
+                if row < t * LANES:
+                    parts = [g[8 * v : 8 * v + 8, :LANES] for g in grams]
+                elif row >= (t + 1) * LANES:
+                    parts = [g[8 * v : 8 * v + 8, LANES:] for g in grams]
+                else:
+                    upper = from_diagonal <= -row
+                    parts = [
+                        jnp.where(upper, g[8 * v : 8 * v + 8, :LANES], g[8 * v : 8 * v + 8, LANES:])
+                        for g in grams
+                    ]
+                value = parts[0] * kw_ref[0]
+                for k in range(1, kpts):
+                    value = value + parts[k] * kw_ref[k]
+                inside = (from_atom >= -row) & (from_atom < NPROJ - row)
+                value = jnp.where(inside, value, 0.0)
+                at = (row // 8) % (FOLD // 8)
+                sums[at] = value if sums[at] is None else sums[at] + value
+            for at, value in enumerate(sums):
+                acc_ref[t, 8 * at : 8 * at + 8, :] = value
+            folded = acc_ref[t, 0:24, :]
+            for q in range(1, FOLD // NPROJ):
+                folded = folded + acc_ref[t, NPROJ * q : NPROJ * q + 24, :]
+            padded = jnp.concatenate([folded, jnp.zeros((LANES - 24, LANES), jnp.float32)], axis=0)
+            y_ref[t * LANES : (t + 1) * LANES, :] = padded.T
+        lane = iota((atoms, LANES), 1)
+        packed = [jnp.zeros((atoms, LANES), jnp.float32) for _ in range(WIDE // LANES)]
+        for j in range(NPROJ):
+            piece = y_ref[pl.ds(j, atoms, stride=NPROJ), :]
+            start = NPROJ * j
+            shift = start % LANES
+            if shift:
+                piece = pltpu.roll(piece, shift, 1)
+            tile = start // LANES
+            here = (lane >= shift) & (lane < shift + NPROJ)
+            packed[tile] = jnp.where(here, piece, packed[tile])
+            if shift + NPROJ > LANES:
+                packed[tile + 1] = jnp.where(lane < shift + NPROJ - LANES, piece, packed[tile + 1])
+        high, low = split(jnp.concatenate(packed, axis=1))
+        parts_ref[s] = jnp.concatenate([high, low], axis=0)
+
+    for s in range(spins):
+        spin_part(s)
+
+    own = own_ref[...]
+    row = jnp.sum(jnp.where(iota(own.shape, 0) == block // 2, own, 0), axis=0, keepdims=True)
+    row = jnp.where(block % 2 == 1, pltpu.roll(row, LANES // 2, 1), row)
+    eye = iota((atoms, LANES), 0) == iota((atoms, LANES), 1)
+    rowf = row.astype(jnp.float32)
+    col = jnp.sum(jnp.where(eye, rowf, 0.0), axis=1, keepdims=True)
+    earlier = (col == rowf) & (iota((atoms, LANES), 0) < iota((atoms, LANES), 1))
+    slot = jnp.sum(jnp.where(earlier, 1.0, 0.0), axis=0, keepdims=True)
+    place = rowf * 4.0 + slot
+    place = jnp.where(iota((1, LANES), 1) < atoms, place, pltpu.roll(place, atoms, 1))
+    out_row = iota((LANES, LANES), 0).astype(jnp.float32)
+    pick = jnp.concatenate(
+        [
+            jnp.where(place + 2.0 * s == out_row, 1.0, 0.0).astype(jnp.bfloat16)
+            for s in range(spins)
+        ],
+        axis=1,
+    )
+    result = dot_f32(pick, parts_ref[...].reshape(spins * LANES, WIDE))
+    for owner in range(out_ref.shape[0]):
+        out_ref[owner] = result[4 * owner : 4 * owner + 4]
 
 
 def gram(index, occupied, kweights, owners, coefficients, interpret=False):
     spins, comps, kpts, bands, columns = coefficients.shape
     tiles = columns // LANES
-    smem = pl.BlockSpec(memory_space=pltpu.SMEM)
+    hbm = pl.BlockSpec(memory_space=pltpu.HBM)
     return pl.pallas_call(
         functools.partial(gram_kernel, index),
-        grid=(spins * kpts,),
-        in_specs=[
-            smem,
-            smem,
-            pl.BlockSpec((4, LANES), lambda g: (0, 0)),
-            pl.BlockSpec((1, comps, 1, bands, columns), lambda g: (g // 2, 0, g % 2, 0, 0)),
-        ],
-        out_specs=pl.BlockSpec((LANES // 4, 4, WIDE), lambda g: (0, 0, 0)),
+        in_specs=[hbm] * 4,
+        out_specs=pl.BlockSpec(memory_space=pltpu.VMEM),
         out_shape=jax.ShapeDtypeStruct((LANES // 4, 4, WIDE), jnp.float32),
         scratch_shapes=[
-            pltpu.VMEM((columns + 2 * EDGE, comps * bands), jnp.bfloat16),
-            pltpu.VMEM((spins, tiles, 80, LANES), jnp.float32),
+            pltpu.SMEM(occupied.shape, jnp.int32),
+            pltpu.SMEM(kweights.shape, jnp.float32),
+            pltpu.VMEM(owners.shape, jnp.int32),
+            pltpu.VMEM(coefficients.shape, jnp.bfloat16),
+            pltpu.VMEM((kpts, columns + 2 * EDGE, comps * bands), jnp.bfloat16),
+            pltpu.VMEM((tiles, 80, LANES), jnp.float32),
             pltpu.VMEM((columns, LANES), jnp.float32),
+            pltpu.VMEM((spins, LANES, WIDE), jnp.bfloat16),
+            pltpu.SemaphoreType.DMA((3, comps, kpts)),
+            pltpu.SemaphoreType.DMA((3,)),
         ],
+        compiler_params=pltpu.CompilerParams(vmem_limit_bytes=GRAM_VMEM),
         cost_estimate=pl.CostEstimate(
-            flops=2 * spins * kpts * columns * 192 * 2 * 2 * bands,
+            flops=2 * spins * kpts * columns * 160 * 2 * 2 * bands,
             bytes_accessed=spins * comps * kpts * bands * columns * 2,
             transcendentals=0,
         ),

time: 73.2 us -> 71.9 us (0.982)
  Pallas kernels: 9.76 us -> 8.41 us
    pallas_call x1, Pallas kernels: 6.71 us -> 5.35 us  [gram(): pl.pallas_call(functools.partial(gram_kernel, index), in_specs=[hbm] * 4,...]
where the time goes in v2:
time: 71.9 us; the launch traced here: 71.7 us
  starting transfers between devices  44.5 us (62%)
  blocking collectives  18 us (25%)
  Pallas kernels  8.41 us (12%)
  between operations  0.76 us (1%)
    all_to_all x1, starting transfers between devices, step(): lax.all_to_all(packed, ('ka', 'ba'), split_axis=0, concat_axis=0, tiled=T...  44.5 us
    psum x1, blocking collectives, step(): sums = lax.psum(sums, 'ga')  18 us
    pallas_call x1, Pallas kernels, gram(): pl.pallas_call(functools.partial(gram_kernel, index), in_specs=[hbm] * 4,...  5.35 us
    pallas_call x1, Pallas kernels, waves(): pl.pallas_call(functools.partial(wave_kernel, index), in_specs=[smem, vme...  2.01 us
  transfers between devices with their start and end apart: 1, of which 0 were waited for; matrix products, arithmetic and copies ran while one was open for 0% of the time, Pallas kernels for 3%

profile of v2, /device:TPU:80, one launch (start us, length us, event | category | flops | bytes accessed | tf_op | source)
XLA Modules:
  0.0 71.7 jit_solution(18178420236248563033)
XLA Ops:
  0.6 0.0 copy-start.1
  0.6 0.0 copy-start.4
  0.7 0.0 copy-start.2
  0.7 0.0 copy-start.6
  0.7 0.0 copy-start
  0.7 0.0 copy-start.3
  0.7 0.0 copy-start.5
  0.7 5.4 %gram.1 = f32[32,4,384]{2,1,0:T(4,128)} custom-call(s32[2,2]{1,0:T(2,128)} %occ_hbm.1, f32[2]{0:T(128)} %kw_hbm.1, s32[4,128]{1,0:T(4,128)} %bitcast.11, bf16[2,2,2,256,1152]{4,3,2,1,0:T(8,128)(2,1)} %x_hbm.1), custom_call_target="tpu_custom_call" | custom-call | flops 1509949440 | bytes 4718592 | tf_op jit(solution)/shard_map/gram/pallas_call | solution.py:238
  6.1 44.5 %all-to-all-start = ((f32[32,4,384]{2,1,0:T(4,128)}), f32[32,4,384]{2,1,0:T(4,128)S(1)}, u32[]{:S(2)}, u32[]{:S(2)}) async-start(f32[32,4,384]{2,1,0:T(4,128)} %gram.1), calls=%async_computation | async-start | bytes 393216 | tf_op jit(solution)/shard_map/all_to_all | solution.py:509
  50.5 0.0 copy-done.4
  50.5 0.0 copy-done.2
  50.6 0.0 copy-done.6
  50.6 0.0 copy-done.3
  50.6 0.0 copy-done.5
  50.6 2.0 %waves.1 = (f32[4,128]{1,0:T(4,128)S(1)}, f32[16,128]{1,0:T(8,128)S(1)}) custom-call(f32[2]{0:T(128)S(1)} %copy-done.6, s32[4,128]{1,0:T(4,128)S(1)} %bitcast.12, s32[4,128]{1,0:T(4,128)S(1)} %bitcast.13, f32[3,512]{1,0:T(4,128)S(1)} %copy-done.3, f32[1728,128]{1,0:T(8,128)S(1)} %bitcast.10), custom_call_target="tpu_custom_call" | custom-call | flops 679477248 | bytes 884736 | tf_op jit(solution)/shard_map/waves/pallas_call | solution.py:412
  52.6 18.0 %psum.7.sums_ref = f32[4,128]{1,0:T(4,128)S(1)} all-reduce(f32[4,128]{1,0:T(4,128)S(1)} %get-tuple-element.17), channel_id=1, replica_groups=mesh['grp'=2,'ka'=16,'ga'=8,'ba'=2] {'ga'}, use_global_device_ids=true, to_apply=%region_0.0 | all-reduce | flops 512 | bytes 4096 | tf_op jit(solution)/shard_map/psum | solution.py:512
  70.6 0.0 all-to-all-done.parts_ref
  70.6 0.0 copy-done.1
  70.6 0.0 copy-done
  70.6 1.0 %final.1 = (f32[2,2,2,324]{3,2,1,0:T(2,128)}, f32[2,3]{1,0:T(2,128)}) custom-call(f32[32,4,384]{2,1,0:T(4,128)S(1)} %all-to-all-done.parts_ref, f32[4,128]{1,0:T(4,128)S(1)} %psum.7.sums_ref, f32[16,128]{1,0:T(8,128)S(1)} %get-tuple-element.18.kinds_ref, f32[9,2,324]{2,1,0:T(2,128)S(1)} %bitcast.9, f32[16,128]{1,0:T(8,128)S(1)} %copy-done.1), custom_call_target="tpu_custom_call" | custom-call | flops 10000000 | bytes 100000 | tf_op jit(solution)/shard_map/final/pallas_call | solution.py:481
Async XLA Ops:
  0.6 70.0 %copy-start.1 = (f32[16,128]{1,0:T(8,128)S(1)}, f32[16,128]{1,0:T(8,128)}, u32[]{:S(2)}) copy-start(f32[16,128]{1,0:T(8,128)} %constant.2.clone.coef_ref) | copy-start | bytes 24580
  0.6 49.9 %copy-start.4 = (s32[512]{0:T(512)S(1)}, s32[512]{0:T(512)}, u32[]{:S(2)}) copy-start(s32[512]{0:T(512)} %param.13) | copy-start | bytes 6148
  0.7 49.9 %copy-start.2 = (f32[2,110592]{1,0:T(2,128)S(1)}, f32[2,110592]{1,0:T(2,128)}, u32[]{:S(2)}) copy-start(f32[2,110592]{1,0:T(2,128)} %param.18) | copy-start | bytes 2654212
  0.7 49.9 %copy-start.6 = (f32[2]{0:T(128)S(1)}, f32[2]{0:T(128)}, u32[]{:S(2)}) copy-start(f32[2]{0:T(128)} %widths_ref) | copy-start | bytes 28
  0.7 69.9 %copy-start = (f32[2,9,324]{2,0,1:T(2,128)S(1)}, f32[2,9,324]{2,0,1:T(2,128)}, u32[]{:S(2)}) copy-start(f32[2,9,324]{2,0,1:T(2,128)} %param.16) | copy-start | bytes 69988
  0.7 49.9 %copy-start.3 = (f32[3,512]{1,0:T(4,128)S(1)}, f32[3,512]{1,0:T(4,128)}, u32[]{:S(2)}) copy-start(f32[3,512]{1,0:T(4,128)} %pos_ref) | copy-start | bytes 18436
  0.7 49.9 %copy-start.5 = (s32[512]{0:T(512)S(1)}, s32[512]{0:T(512)}, u32[]{:S(2)}) copy-start(s32[512]{0:T(512)} %param.14) | copy-start | bytes 6148
  6.1 64.5 %all-to-all-start = ((f32[32,4,384]{2,1,0:T(4,128)}), f32[32,4,384]{2,1,0:T(4,128)S(1)}, u32[]{:S(2)}, u32[]{:S(2)}) async-start(f32[32,4,384]{2,1,0:T(4,128)} %gram.1), calls=%async_computation | async-start | bytes 393216 | tf_op jit(solution)/shard_map/all_to_all | solution.py:509

commit v3 on v2

--- a/solution.py
+++ b/solution.py
@@ -25,6 +25,7 @@
 ]
 MONO_PAD = 32
 GRAM_VMEM = 60 << 20
+CHUNKS = 2
 FIRST = 4
 
 
@@ -50,6 +51,13 @@
     return table
 
 
+def swap_table():
+    table = np.zeros((WIDE, WIDE), np.float32)
+    e = np.arange(PACKED)
+    table[e, e % NPROJ * NPROJ + e // NPROJ] = 1.0
+    return table
+
+
 def iota(shape, dim):
     return lax.broadcasted_iota(jnp.int32, shape, dim)
 
@@ -108,6 +116,18 @@
         copy.wait()
     atoms = LANES // 2
 
+    waited = set()
+
+    def arrived(s, t):
+        for n, cut in enumerate(cuts):
+            if cut[:2] == (s, t) and n not in waited:
+                waited.add(n)
+                for copy in arrivals(n):
+                    copy.wait()
+                if n == 0:
+                    for copy in arrivals(2):
+                        copy.start()
+
     def spin_part(s):
         band = iota((1, comps * bands), 1) % bands
         masks = [
@@ -123,20 +143,11 @@
                 )
                 xt_ref[k, EDGE + t * LANES : EDGE + (t + 1) * LANES, :] = block_t * masks[k]
 
-        def arrived(t):
-            for n, cut in enumerate(cuts):
-                if cut[:2] == (s, t):
-                    for copy in arrivals(n):
-                        copy.wait()
-                    if n == 0:
-                        for copy in arrivals(2):
-                            copy.start()
-
-        arrived(0)
+        arrived(s, 0)
         turned(0)
         for t in range(tiles):
             if t + 1 < tiles:
-                arrived(t + 1)
+                arrived(s, t + 1)
                 turned(t + 1)
             lane = iota((8, LANES), 1) + t * LANES
             rows = iota((8, LANES), 0)
@@ -317,7 +328,7 @@
         for c in range(3)
     ]
     kind = on_lanes(spread(species_ref[...]).astype(jnp.float32))
-    width = jnp.where(kind > 0.5, widths_ref[1], widths_ref[0])
+    width = jnp.where(kind > 0.5, widths_ref[0:1, 1:2], widths_ref[0:1, 0:1])
     turns = [p * np.float32(grid_step / (2.0 * np.pi)) for p in place]
 
     def power(g, exponent):
@@ -337,16 +348,27 @@
         shift = jnp.where(imag == 0, 0.25 + 0.25 * c, 0.25 * c)
         h, l = split(sin_turns(phase + shift) * factor)
         for line in range(lines):
-            r = c * WIDE + line * GRID
-            uh_ref[r : r + GRID, line * LANES : (line + 1) * LANES] = h
-            ul_ref[r : r + GRID, line * LANES : (line + 1) * LANES] = l
-
-    pieces = [
-        split(pot_ref[pl.ds(2 * k + c, rows, stride=6), :]) for c in range(2) for k in range(3)
-    ]
-    vh = jnp.concatenate([p[0] for p in pieces], axis=1)
-    vl = jnp.concatenate([p[1] for p in pieces], axis=1)
-    first = dot_f32(vh, uh_ref[...]) + dot_f32(vl, uh_ref[...]) + dot_f32(vh, ul_ref[...])
+            side, place_in = line // 2, line % 2
+            r = c * 2 * LANES + line * GRID - side * LANES
+            n = place_in * LANES
+            uh_ref[side, r : r + GRID, n : n + LANES] = h
+            ul_ref[side, r : r + GRID, n : n + LANES] = l
+
+    def lines_of(low, high):
+        pieces = [
+            [
+                split(pot_ref[pl.ds(2 * k + c + 6 * low, high - low, stride=6), :])
+                for k in range(3)
+            ]
+            for c in range(2)
+        ]
+        sides = []
+        for side in range(2):
+            vh = jnp.concatenate([pieces[c][side + k][0] for c in range(2) for k in range(2)], axis=1)
+            vl = jnp.concatenate([pieces[c][side + k][1] for c in range(2) for k in range(2)], axis=1)
+            uh, ul = uh_ref[side], ul_ref[side]
+            sides.append(dot_f32(vh, uh) + dot_f32(vl, uh) + dot_f32(vh, ul))
+        return jnp.concatenate(sides, axis=1)
 
     def tiled(a):
         return jnp.concatenate([a] * lines, axis=1)
@@ -370,9 +392,13 @@
     zc = sin_turns(phase + 0.25) * damp
 
     sums = {}
+    chunk = planes // CHUNKS
     for z in range(planes):
+        if z % chunk == 0:
+            first = lines_of(z * group, (z + chunk) * group)
         wave = y1 * tiled(zc[z : z + 1]) + y2 * tiled(zs[z : z + 1])
-        term = first[z * group : (z + 1) * group] * wave
+        row = z % chunk * group
+        term = first[row : row + group] * wave
         gz_row = gz[z : z + 1]
         for b in range(4):
             if b:
@@ -407,35 +433,31 @@
 
 
 def waves(index, widths, owners, species, positions, potential, interpret=False):
-    smem = pl.BlockSpec(memory_space=pltpu.SMEM)
     vmem = pl.BlockSpec(memory_space=pltpu.VMEM)
     return pl.pallas_call(
         functools.partial(wave_kernel, index),
-        in_specs=[smem, vmem, vmem, vmem, vmem],
+        in_specs=[vmem] * 5,
         out_specs=(vmem, vmem),
         out_shape=(
             jax.ShapeDtypeStruct((4, LANES), jnp.float32),
             jax.ShapeDtypeStruct((16, LANES), jnp.float32),
         ),
-        scratch_shapes=[pltpu.VMEM((2 * WIDE, 4 * LANES), jnp.bfloat16)] * 2,
+        scratch_shapes=[pltpu.VMEM((2, 4 * LANES, 2 * LANES), jnp.bfloat16)] * 2,
         cost_estimate=pl.CostEstimate(
             flops=2 * 288 * 768 * 512 * 3, bytes_accessed=potential.size * 4, transcendentals=0
         ),
         compiler_params=pltpu.CompilerParams(vmem_limit_bytes=16 << 20),
         name="waves",
         interpret=interpret,
-    )(widths, owners, species, positions, potential)
-
-
-def final_kernel(index, parts_ref, sums_ref, kinds_ref, mult_ref, coef_ref, density_ref, forces_ref):
+    )(widths.reshape(1, -1), owners, species, positions, potential)
+
+
+def final_kernel(index, parts_ref, sums_ref, kinds_ref, swap_ref, mult_ref, coef_ref, density_ref, forces_ref):
     total = parts_ref[0]
     for r in range(1, parts_ref.shape[0]):
         total = total + parts_ref[r]
     z = jnp.concatenate([total, total], axis=0)
-    r = iota((WIDE, WIDE), 0)
-    u = div18(r)
-    swap = (iota((WIDE, WIDE), 1) == (r - NPROJ * u) * NPROJ + u) & (r < PACKED)
-    swap = jnp.where(swap, 1.0, 0.0).astype(jnp.bfloat16)
+    swap = swap_ref[...]
     high = z.astype(jnp.bfloat16)
     rest = z - high.astype(jnp.float32)
     middle = rest.astype(jnp.bfloat16)
@@ -476,11 +498,11 @@
     forces_ref[...] = forces[0:2, :]
 
 
-def final(index, parts, sums, kinds, multipole, coefs, interpret=False):
+def final(index, parts, sums, kinds, swap, multipole, coefs, interpret=False):
     vmem = pl.BlockSpec(memory_space=pltpu.VMEM)
     return pl.pallas_call(
         functools.partial(final_kernel, index),
-        in_specs=[vmem] * 5,
+        in_specs=[vmem] * 6,
         out_specs=(vmem, vmem),
         out_shape=(
             jax.ShapeDtypeStruct((2, 2, 2, PACKED), jnp.float32),
@@ -490,7 +512,7 @@
         compiler_params=pltpu.CompilerParams(vmem_limit_bytes=8 << 20),
         name="final",
         interpret=interpret,
-    )(parts, sums, kinds, multipole, coefs)
+    )(parts, sums, kinds, swap, multipole, coefs)
 
 
 def place():
@@ -511,7 +533,13 @@
     sums, kinds = waves(place, widths, owners, species.reshape(4, LANES), positions, values)
     sums = lax.psum(sums, "ga")
     density, forces = final(
-        place, arrived, sums, kinds, multipole.transpose(1, 0, 2), jnp.asarray(force_coefficients())
+        place,
+        arrived,
+        sums,
+        kinds,
+        jnp.asarray(swap_table(), jnp.bfloat16),
+        multipole.transpose(1, 0, 2),
+        jnp.asarray(force_coefficients()),
     )
     return density, forces.T
 

time: 71.9 us -> 71.4 us (level)
  Pallas kernels: 8.41 us -> 7.63 us
    pallas_call x1, Pallas kernels: 2.01 us -> 1.24 us  [waves(): pl.pallas_call(functools.partial(wave_kernel, index), in_specs=[vmem] * 5...]
  transfers between devices with their start and end apart: 1 -> 1, of which waited for: 0 -> 0; matrix products, arithmetic and copies ran while one was open for 0% -> 0% of each run, Pallas kernels for 3% -> 2%
where the time goes in v3:
time: 71.4 us; the launch traced here: 70.9 us
  starting transfers between devices  44.5 us (62%)
  blocking collectives  18 us (25%)
  Pallas kernels  7.63 us (11%)
  between operations  0.77 us (1%)
    all_to_all x1, starting transfers between devices, step(): lax.all_to_all(packed, ('ka', 'ba'), split_axis=0, concat_axis=0, tiled=T...  44.5 us
    psum x1, blocking collectives, step(): sums = lax.psum(sums, 'ga')  18 us
    pallas_call x1, Pallas kernels, gram(): pl.pallas_call(functools.partial(gram_kernel, index), in_specs=[hbm] * 4,...  5.37 us
  transfers between devices with their start and end apart: 1, of which 0 were waited for; matrix products, arithmetic and copies ran while one was open for 0% of the time, Pallas kernels for 2%

profile of v3, /device:TPU:80, one launch (start us, length us, event | category | flops | bytes accessed | tf_op | source)
XLA Modules:
  0.0 70.9 jit_solution(10668698800683959898)
XLA Ops:
  0.6 0.0 copy-start.2
  0.6 0.0 copy-start
  0.7 0.0 copy-start.5
  0.7 0.0 copy-start.3
  0.7 0.0 copy-start.7
  0.7 0.0 copy-start.1
  0.7 0.0 copy-start.4
  0.7 0.0 copy-start.6
  0.7 5.4 %gram.1 = f32[32,4,384]{2,1,0:T(4,128)} custom-call(s32[2,2]{1,0:T(2,128)} %occ_hbm.1, f32[2]{0:T(128)} %kw_hbm.1, s32[4,128]{1,0:T(4,128)} %bitcast.12, bf16[2,2,2,256,1152]{4,3,2,1,0:T(8,128)(2,1)} %x_hbm.1), custom_call_target="tpu_custom_call" | custom-call | flops 1509949440 | bytes 4718592 | tf_op jit(solution)/shard_map/gram/pallas_call | solution.py:249
  6.1 44.5 %all-to-all-start = ((f32[32,4,384]{2,1,0:T(4,128)}), f32[32,4,384]{2,1,0:T(4,128)S(1)}, u32[]{:S(2)}, u32[]{:S(2)}) async-start(f32[32,4,384]{2,1,0:T(4,128)} %gram.1), calls=%async_computation | async-start | bytes 393216 | tf_op jit(solution)/shard_map/all_to_all | solution.py:531
  50.6 0.0 copy-done.5
  50.6 0.0 copy-done.3
  50.6 0.0 copy-done.7
  50.6 0.0 copy-done.4
  50.6 0.0 copy-done.6
  50.6 1.2 %waves.1 = (f32[4,128]{1,0:T(4,128)S(1)}, f32[16,128]{1,0:T(8,128)S(1)}) custom-call(f32[1,2]{1,0:T(1,128)S(1)} %bitcast.15, s32[4,128]{1,0:T(4,128)S(1)} %bitcast.13, s32[4,128]{1,0:T(4,128)S(1)} %bitcast.14, f32[3,512]{1,0:T(4,128)S(1)} %copy-done.4, f32[1728,128]{1,0:T(8,128)S(1)} %bitcast.11), custom_call_target="tpu_custom_call" | custom-call | flops 679477248 | bytes 884736 | tf_op jit(solution)/shard_map/waves/pallas_call | solution.py:437
  51.9 18.0 %psum.7.sums_ref = f32[4,128]{1,0:T(4,128)S(1)} all-reduce(f32[4,128]{1,0:T(4,128)S(1)} %get-tuple-element.17), channel_id=1, replica_groups=mesh['grp'=2,'ka'=16,'ga'=8,'ba'=2] {'ga'}, use_global_device_ids=true, to_apply=%region_0.0 | all-reduce | flops 512 | bytes 4096 | tf_op jit(solution)/shard_map/psum | solution.py:534
  69.9 0.0 all-to-all-done.parts_ref
  69.9 0.0 copy-done.2
  69.9 0.0 copy-done
  69.9 0.0 copy-done.1
  69.9 1.0 %final.1 = (f32[2,2,2,324]{3,2,1,0:T(2,128)}, f32[2,3]{1,0:T(2,128)}) custom-call(f32[32,4,384]{2,1,0:T(4,128)S(1)} %all-to-all-done.parts_ref, f32[4,128]{1,0:T(4,128)S(1)} %psum.7.sums_ref, f32[16,128]{1,0:T(8,128)S(1)} %get-tuple-element.18.kinds_ref, bf16[384,384]{1,0:T(8,128)(2,1)S(1)} %copy-done, f32[9,2,324]{2,1,0:T(2,128)S(1)} %bitcast.10, ...), custom_call_target="tpu_custom_call" | custom-call | flops 10000000 | bytes 100000 | tf_op jit(solution)/shard_map/final/pallas_call | solution.py:503
Async XLA Ops:
  0.6 69.3 %copy-start.2 = (f32[16,128]{1,0:T(8,128)S(1)}, f32[16,128]{1,0:T(8,128)}, u32[]{:S(2)}) copy-start(f32[16,128]{1,0:T(8,128)} %constant.5.clone.coef_ref) | copy-start | bytes 24580
  0.6 69.2 %copy-start = (bf16[384,384]{1,0:T(8,128)(2,1)S(1)}, bf16[384,384]{1,0:T(8,128)(2,1)}, u32[]{:S(2)}) copy-start(bf16[384,384]{1,0:T(8,128)(2,1)} %constant.4.clone.swap_ref) | copy-start | bytes 884740
  0.7 49.9 %copy-start.5 = (s32[512]{0:T(512)S(1)}, s32[512]{0:T(512)}, u32[]{:S(2)}) copy-start(s32[512]{0:T(512)} %param.14) | copy-start | bytes 6148
  0.7 49.9 %copy-start.3 = (f32[2,110592]{1,0:T(2,128)S(1)}, f32[2,110592]{1,0:T(2,128)}, u32[]{:S(2)}) copy-start(f32[2,110592]{1,0:T(2,128)} %param.19) | copy-start | bytes 2654212
  0.7 49.9 %copy-start.7 = (f32[2]{0:T(128)S(1)}, f32[2]{0:T(128)}, u32[]{:S(2)}) copy-start(f32[2]{0:T(128)} %param.18) | copy-start | bytes 28
  0.7 69.2 %copy-start.1 = (f32[2,9,324]{2,0,1:T(2,128)S(1)}, f32[2,9,324]{2,0,1:T(2,128)}, u32[]{:S(2)}) copy-start(f32[2,9,324]{2,0,1:T(2,128)} %param.17) | copy-start | bytes 69988
  0.7 49.9 %copy-start.4 = (f32[3,512]{1,0:T(4,128)S(1)}, f32[3,512]{1,0:T(4,128)}, u32[]{:S(2)}) copy-start(f32[3,512]{1,0:T(4,128)} %pos_ref) | copy-start | bytes 18436
  0.7 49.9 %copy-start.6 = (s32[512]{0:T(512)S(1)}, s32[512]{0:T(512)}, u32[]{:S(2)}) copy-start(s32[512]{0:T(512)} %param.15) | copy-start | bytes 6148
  6.1 63.8 %all-to-all-start = ((f32[32,4,384]{2,1,0:T(4,128)}), f32[32,4,384]{2,1,0:T(4,128)S(1)}, u32[]{:S(2)}, u32[]{:S(2)}) async-start(f32[32,4,384]{2,1,0:T(4,128)} %gram.1), calls=%async_computation | async-start | bytes 393216 | tf_op jit(solution)/shard_map/all_to_all | solution.py:531

commit v4 on v3

--- a/solution.py
+++ b/solution.py
@@ -24,6 +24,8 @@
     (a, b, c) for a in range(4) for b in range(4) for c in range(4) if a + b + c <= 3
 ]
 MONO_PAD = 32
+REST = PACKED - 2 * LANES
+LINES = 11
 GRAM_VMEM = 60 << 20
 CHUNKS = 2
 FIRST = 4
@@ -227,19 +229,34 @@
     col = jnp.sum(jnp.where(eye, rowf, 0.0), axis=1, keepdims=True)
     earlier = (col == rowf) & (iota((atoms, LANES), 0) < iota((atoms, LANES), 1))
     slot = jnp.sum(jnp.where(earlier, 1.0, 0.0), axis=0, keepdims=True)
-    place = rowf * 4.0 + slot
+    place = slot * 32.0 + rowf
     place = jnp.where(iota((1, LANES), 1) < atoms, place, pltpu.roll(place, atoms, 1))
     out_row = iota((LANES, LANES), 0).astype(jnp.float32)
     pick = jnp.concatenate(
         [
-            jnp.where(place + 2.0 * s == out_row, 1.0, 0.0).astype(jnp.bfloat16)
+            jnp.where(place + 64.0 * s == out_row, 1.0, 0.0).astype(jnp.bfloat16)
             for s in range(spins)
         ],
         axis=1,
     )
     result = dot_f32(pick, parts_ref[...].reshape(spins * LANES, WIDE))
-    for owner in range(out_ref.shape[0]):
-        out_ref[owner] = result[4 * owner : 4 * owner + 4]
+    owners = LANES // 4
+    quarters = [result[owners * q : owners * (q + 1)] for q in range(4)]
+    a0, a1, a2, a3 = [r[:, 2 * LANES :] for r in quarters]
+    lane = iota((owners, LANES), 1)
+    a1, a3 = pltpu.roll(a1, REST, 1), pltpu.roll(a3, 2 * REST - LANES + REST, 1)
+    lines = [r[:, :LANES] for r in quarters] + [r[:, LANES : 2 * LANES] for r in quarters]
+    lines += [
+        jnp.where(lane < REST, a0, a1),
+        jnp.where(
+            lane < 2 * REST - LANES,
+            a1,
+            jnp.where(lane < 3 * REST - LANES, pltpu.roll(a2, 2 * REST - LANES, 1), a3),
+        ),
+        jnp.where(lane < 4 * REST - 2 * LANES, a3, 0.0),
+    ]
+    for n, line in enumerate(lines):
+        out_ref[pl.ds(n, owners, stride=LINES), :] = line
 
 
 def gram(index, occupied, kweights, owners, coefficients, interpret=False):
@@ -250,7 +267,7 @@
         functools.partial(gram_kernel, index),
         in_specs=[hbm] * 4,
         out_specs=pl.BlockSpec(memory_space=pltpu.VMEM),
-        out_shape=jax.ShapeDtypeStruct((LANES // 4, 4, WIDE), jnp.float32),
+        out_shape=jax.ShapeDtypeStruct((LANES // 4 * LINES, LANES), jnp.float32),
         scratch_shapes=[
             pltpu.SMEM(occupied.shape, jnp.int32),
             pltpu.SMEM(kweights.shape, jnp.float32),
@@ -453,10 +470,32 @@
 
 
 def final_kernel(index, parts_ref, sums_ref, kinds_ref, swap_ref, mult_ref, coef_ref, density_ref, forces_ref):
-    total = parts_ref[0]
-    for r in range(1, parts_ref.shape[0]):
-        total = total + parts_ref[r]
-    z = jnp.concatenate([total, total], axis=0)
+    senders = parts_ref.shape[0] // LINES
+    sums_of = [
+        jnp.sum(parts_ref[pl.ds(n, senders, stride=LINES), :], axis=0, keepdims=True)
+        for n in range(LINES)
+    ]
+    lane = iota((1, LANES), 1)
+    l8, l9, l10 = sums_of[8:]
+    cut = 2 * LANES - 3 * REST
+    ends = [
+        l8,
+        jnp.where(
+            lane < LANES - REST, pltpu.roll(l8, LANES - REST, 1), pltpu.roll(l9, LANES - REST, 1)
+        ),
+        pltpu.roll(l9, 2 * LANES - 2 * REST, 1),
+        jnp.where(lane < cut, pltpu.roll(l9, cut, 1), pltpu.roll(l10, cut, 1)),
+    ]
+    ends = [jnp.where(lane < REST, end, 0.0) for end in ends]
+    at = iota((8, LANES), 0) % 4
+
+    def stacked(rows):
+        out = rows[3]
+        for q in range(3):
+            out = jnp.where(at == q, rows[q], out)
+        return out
+
+    z = jnp.concatenate([stacked(sums_of[0:4]), stacked(sums_of[4:8]), stacked(ends)], axis=1)
     swap = swap_ref[...]
     high = z.astype(jnp.bfloat16)
     rest = z - high.astype(jnp.float32)
@@ -528,7 +567,9 @@
     packed, widths, positions, species, potential, multipole = lax.optimization_barrier(
         (packed, widths, positions, species, potential, multipole)
     )
+    packed = packed.reshape(-1, LINES, 1, LANES)
     arrived = lax.all_to_all(packed, ("ka", "ba"), split_axis=0, concat_axis=0, tiled=True)
+    arrived = arrived.reshape(-1, LANES)
     values = potential.reshape(2, -1, LANES).transpose(1, 0, 2).reshape(-1, LANES)
     sums, kinds = waves(place, widths, owners, species.reshape(4, LANES), positions, values)
     sums = lax.psum(sums, "ga")

time: 71.4 us -> 71.6 us (level)
  no operation moved by 1% of the time
where the time goes in v4:
time: 71.6 us; the launch traced here: 71.4 us
  starting transfers between devices  44.5 us (62%)
  blocking collectives  18 us (25%)
  Pallas kernels  8.07 us (11%)
  between operations  0.77 us (1%)
    all_to_all x1, starting transfers between devices, step(): lax.all_to_all(packed, ('ka', 'ba'), split_axis=0, concat_axis=0, tiled=T...  44.5 us
    psum x1, blocking collectives, step(): sums = lax.psum(sums, 'ga')  18 us
    pallas_call x1, Pallas kernels, gram(): pl.pallas_call(functools.partial(gram_kernel, index), in_specs=[hbm] * 4,...  5.77 us
  transfers between devices with their start and end apart: 1, of which 0 were waited for; matrix products, arithmetic and copies ran while one was open for 0% of the time, Pallas kernels for 2%

profile of v4, /device:TPU:80, one launch (start us, length us, event | category | flops | bytes accessed | tf_op | source)
XLA Modules:
  0.0 71.4 jit_solution(9804592394991880491)
XLA Ops:
  0.6 0.0 copy-start.2
  0.6 0.0 copy-start
  0.7 0.0 copy-start.5
  0.7 0.0 copy-start.3
  0.7 0.0 copy-start.7
  0.7 0.0 copy-start.1
  0.7 0.0 copy-start.4
  0.7 0.0 copy-start.6
  0.7 5.8 %gram.1 = f32[352,128]{1,0:T(8,128)} custom-call(s32[2,2]{1,0:T(2,128)} %occ_hbm.1, f32[2]{0:T(128)} %kw_hbm.1, s32[4,128]{1,0:T(4,128)} %bitcast.15, bf16[2,2,2,256,1152]{4,3,2,1,0:T(8,128)(2,1)} %x_hbm.1), custom_call_target="tpu_custom_call" | custom-call | flops 1509949440 | bytes 4718592 | tf_op jit(solution)/shard_map/gram/pallas_call | solution.py:266
  6.5 44.5 %all-to-all-start = ((f32[32,11,1,128]{3,2,1,0:T(1,128)}), f32[32,11,1,128]{3,2,1,0:T(1,128)S(1)}, u32[]{:S(2)}, u32[]{:S(2)}) async-start(f32[32,11,1,128]{3,2,1,0:T(1,128)} %bitcast.19), calls=%async_computation | async-start | bytes 360448 | tf_op jit(solution)/shard_map/all_to_all | solution.py:571
  51.0 0.0 copy-done.5
  51.0 0.0 copy-done.3
  51.0 0.0 copy-done.7
  51.0 0.0 copy-done.4
  51.0 0.0 copy-done.6
  51.0 1.2 %waves.1 = (f32[4,128]{1,0:T(4,128)S(1)}, f32[16,128]{1,0:T(8,128)S(1)}) custom-call(f32[1,2]{1,0:T(1,128)S(1)} %bitcast.18, s32[4,128]{1,0:T(4,128)S(1)} %bitcast.16, s32[4,128]{1,0:T(4,128)S(1)} %bitcast.17, f32[3,512]{1,0:T(4,128)S(1)} %copy-done.4, f32[1728,128]{1,0:T(8,128)S(1)} %bitcast.14), custom_call_target="tpu_custom_call" | custom-call | flops 679477248 | bytes 884736 | tf_op jit(solution)/shard_map/waves/pallas_call | solution.py:454
  52.3 18.0 %psum.7.sums_ref = f32[4,128]{1,0:T(4,128)S(1)} all-reduce(f32[4,128]{1,0:T(4,128)S(1)} %get-tuple-element.17), channel_id=1, replica_groups=mesh['grp'=2,'ka'=16,'ga'=8,'ba'=2] {'ga'}, use_global_device_ids=true, to_apply=%region_0.0 | all-reduce | flops 512 | bytes 4096 | tf_op jit(solution)/shard_map/psum | solution.py:575
  70.3 0.0 all-to-all-done
  70.3 0.0 copy-done.2
  70.3 0.0 copy-done
  70.3 0.0 copy-done.1
  70.3 1.0 %final.1 = (f32[2,2,2,324]{3,2,1,0:T(2,128)}, f32[2,3]{1,0:T(2,128)}) custom-call(f32[352,128]{1,0:T(8,128)S(1)} %bitcast.12, f32[4,128]{1,0:T(4,128)S(1)} %psum.7.sums_ref, f32[16,128]{1,0:T(8,128)S(1)} %get-tuple-element.18.kinds_ref, bf16[384,384]{1,0:T(8,128)(2,1)S(1)} %copy-done, f32[9,2,324]{2,1,0:T(2,128)S(1)} %bitcast.13, f32[16,128]{1,0:T(8,128)S(1)} %copy-done.2), custom_call_target="tpu_custom_call" | custom-call | flops 10000000 | bytes 100000 | tf_op jit(solution)/shard_map/final/pallas_call | solution.py:542
Async XLA Ops:
  0.6 69.7 %copy-start.2 = (f32[16,128]{1,0:T(8,128)S(1)}, f32[16,128]{1,0:T(8,128)}, u32[]{:S(2)}) copy-start(f32[16,128]{1,0:T(8,128)} %constant.5.clone.coef_ref) | copy-start | bytes 24580
  0.6 69.6 %copy-start = (bf16[384,384]{1,0:T(8,128)(2,1)S(1)}, bf16[384,384]{1,0:T(8,128)(2,1)}, u32[]{:S(2)}) copy-start(bf16[384,384]{1,0:T(8,128)(2,1)} %constant.4.clone.swap_ref) | copy-start | bytes 884740
  0.7 50.3 %copy-start.5 = (s32[512]{0:T(512)S(1)}, s32[512]{0:T(512)}, u32[]{:S(2)}) copy-start(s32[512]{0:T(512)} %param.14) | copy-start | bytes 6148
  0.7 50.3 %copy-start.3 = (f32[2,110592]{1,0:T(2,128)S(1)}, f32[2,110592]{1,0:T(2,128)}, u32[]{:S(2)}) copy-start(f32[2,110592]{1,0:T(2,128)} %param.19) | copy-start | bytes 2654212
  0.7 50.3 %copy-start.7 = (f32[2]{0:T(128)S(1)}, f32[2]{0:T(128)}, u32[]{:S(2)}) copy-start(f32[2]{0:T(128)} %param.18) | copy-start | bytes 28
  0.7 69.6 %copy-start.1 = (f32[2,9,324]{2,0,1:T(2,128)S(1)}, f32[2,9,324]{2,0,1:T(2,128)}, u32[]{:S(2)}) copy-start(f32[2,9,324]{2,0,1:T(2,128)} %param.17) | copy-start | bytes 69988
  0.7 50.3 %copy-start.4 = (f32[3,512]{1,0:T(4,128)S(1)}, f32[3,512]{1,0:T(4,128)}, u32[]{:S(2)}) copy-start(f32[3,512]{1,0:T(4,128)} %pos_ref) | copy-start | bytes 18436
  0.7 50.3 %copy-start.6 = (s32[512]{0:T(512)S(1)}, s32[512]{0:T(512)}, u32[]{:S(2)}) copy-start(s32[512]{0:T(512)} %param.15) | copy-start | bytes 6148
  6.5 63.8 %all-to-all-start = ((f32[32,11,1,128]{3,2,1,0:T(1,128)}), f32[32,11,1,128]{3,2,1,0:T(1,128)S(1)}, u32[]{:S(2)}, u32[]{:S(2)}) async-start(f32[32,11,1,128]{3,2,1,0:T(1,128)} %bitcast.19), calls=%async_computation | async-start | bytes 360448 | tf_op jit(solution)/shard_map/all_to_all | solution.py:571
